TPU v7x, 128 devices: a whole 4x4x4 slice. The times are simulated.
128 devices in a mesh: rows: 16 (over x, z), cols: 8 (over y, core).
Axes of the slice: x: 4, y: 4, z: 4, core: 2. Of those that a mesh axis runs over, the one named last changes fastest.
Arguments:
- bag_index: int32 [2048, 128], P(('rows', 'cols')), may hold values from 0 to 1048575, as said below
- bag_length: int32 [2048, 4], P(('rows', 'cols')), may hold values from 1 to 32
- emb_tables: float32 [4, 1048576, 128], P(None, ('rows', 'cols')), may hold values from -0.6 to 0.6
- dense_feats: float32 [2048, 128], P(('rows', 'cols')), may hold values from -6 to 6
- w_dense: float32 [128, 1024], replicated, may hold values from -0.5 to 0.5
- w_pair: float32 [10, 1024], replicated, may hold values from -0.5 to 0.5
- top_bias: float32 [1024], replicated, may hold values from -3 to 3
Outputs:
- pooled: float32 [2048, 4, 128], P(('rows', 'cols'))
- top_hidden: float32 [2048, 1024], P(('rows', 'cols'))
Inputs may be any that keep to these rules, and one draw needn't show every extreme that they name: `bag_length`: slots at or past a bag's length are ignored, whatever they hold. `bag_index`: device d holds rows d * 8192 to (d + 1) * 8192 - 1 of every table; among the 2048 slots (live or not) of the samples of one device, at most 32 hold rows of any one device, and in every draw some device's rows receive exactly 32 slots from every device.
All inputs are finite; a program needn't handle non-finite values.
Results may differ from a plain program's by a relative error of at most 0.0001.
Values sent between devices are 32-bit elements; how exact they have to be, the bound alone decides.
No kernel may reach another device: no remote copies, remote signals or barrier semaphores. Data moves between devices by JAX's collectives and lax.ppermute only.
A program may use at most 128 MiB of HBM per device.

v0:
```python
import jax
import jax.numpy as jnp
from jax import lax
from jax.sharding import PartitionSpec as P

NT = 4
L = 32


def interact(dense_feats, pooled, w_dense, w_pair, top_bias):
    feats = [dense_feats] + [pooled[:, t, :] for t in range(NT)]
    pair_list = []
    for first in range(NT + 1):
        for second in range(first + 1, NT + 1):
            pair_list.append(jnp.sum(feats[first] * feats[second], axis=-1))
    pair_dots = jnp.stack(pair_list, axis=1)
    hidden = jnp.dot(
        dense_feats, w_dense, precision=lax.Precision.HIGHEST, preferred_element_type=jnp.float32
    )
    hidden = hidden + jnp.dot(
        pair_dots, w_pair, precision=lax.Precision.HIGHEST, preferred_element_type=jnp.float32
    )
    return jnp.maximum(hidden + top_bias, 0.0)


def shards(bag_index, bag_length, emb_tables, dense_feats, w_dense, w_pair, top_bias):
    samples = bag_index.shape[0]
    local_rows = emb_tables.shape[1]
    width = emb_tables.shape[2]
    position = jnp.arange(L, dtype=jnp.int32)
    devices = lax.axis_size("rows") * lax.axis_size("cols")
    slots = samples * NT * L
    capacity = 2 * slots // devices
    flat_ids = bag_index.reshape(slots)
    target = flat_ids // local_rows
    slot_iota = jnp.arange(slots, dtype=jnp.int32)
    table_of = slot_iota % (NT * L) // L
    code = table_of * local_rows + flat_ids - target * local_rows
    earlier = (slot_iota[None, :] < slot_iota[:, None]) & (target[None, :] == target[:, None])
    rank = jnp.sum(earlier.astype(jnp.int32), axis=1)
    owner_hot = (target[:, None] == jnp.arange(devices, dtype=jnp.int32)[None, :]).astype(
        jnp.float32
    )
    rank_hot = (rank[:, None] == jnp.arange(capacity, dtype=jnp.int32)[None, :]).astype(jnp.float32)
    weighted = owner_hot * code.astype(jnp.float32)[:, None]
    outbox = jnp.einsum(
        "sd,sc->dc",
        weighted,
        rank_hot,
        precision=lax.Precision.HIGHEST,
        preferred_element_type=jnp.float32,
    )
    outbox = outbox.astype(jnp.int32)
    flat_table = emb_tables.reshape(NT * local_rows, width)
    found = jnp.take(
        flat_table,
        lax.all_to_all(outbox, ("rows", "cols"), split_axis=0, concat_axis=0, tiled=True),
        axis=0,
    )
    fetched = lax.all_to_all(found, ("rows", "cols"), split_axis=0, concat_axis=0, tiled=True)
    place = target * capacity + rank
    selector = (place[:, None] == jnp.arange(devices * capacity, dtype=jnp.int32)[None, :]).astype(
        jnp.float32
    )
    picked = jnp.dot(
        selector,
        fetched.reshape(devices * capacity, width),
        precision=lax.Precision.HIGHEST,
        preferred_element_type=jnp.float32,
    )
    picked = picked.reshape(samples, NT, L, width)
    live = position[None, None, :] < bag_length[:, :, None]
    pooled = jnp.sum(jnp.where(live[:, :, :, None], picked, 0.0), axis=2)
    return (pooled, interact(dense_feats, pooled, w_dense, w_pair, top_bias))


def solution(mesh):
    in_specs = (
        P(("rows", "cols"), None),
        P(("rows", "cols"), None),
        P(None, ("rows", "cols"), None),
        P(("rows", "cols"), None),
        P(),
        P(),
        P(),
    )
    out_specs = (P(("rows", "cols"), None, None), P(("rows", "cols"), None))
    return jax.shard_map(shards, mesh=mesh, in_specs=in_specs, out_specs=out_specs, check_vma=False)
```

profile of v0, /device:TPU:1, one launch (start us, length us, event | category | flops | bytes accessed | tf_op | source)
XLA Modules:
  0.0 99.4 jit_solution(9859492654781708526)
XLA Ops:
  0.6 0.0 copy-start
  0.6 0.8 fusion.28
  1.4 4.6 %convert_reduce_fusion = s32[2048]{0:T(1024)S(1)} fusion(s32[2048]{0:T(1024)S(1)} %get-tuple-element.17), kind=kLoop, calls=%fused_computation.5 | loop fusion | flops 20969472 | bytes 16384 | tf_op jit(solution)/shard_map/reduce_sum | solution.py:40
  6.0 1.9 %fusion.13 = s32[128,1,32]{0,2,1:T(8,128)S(1)} fusion(s32[2048]{0:T(1024)S(1)} %convert_reduce_fusion, f32[2048]{0:T(1024)S(1)} %get-tuple-element.16, s32[2048]{0:T(1024)S(1)} %get-tuple-element.17), kind=kOutput, calls=%fused_computation.14 | convolution fusion | flops 101257216 | bytes 40960 | tf_op jit(solution)/shard_map/sd,sc->dc/dot_general | solution.py:46
  7.9 0.1 copy.26
  8.0 20.8 %all_to_all.20 = s32[128,1,32]{2,1,0:T(1,128)S(1)} all-to-all(s32[128,1,32]{2,1,0:T(1,128)S(1)} %copy.26), channel_id=1, replica_groups=mesh['rows'=16,'cols'=8] {'rows','cols'}, dimensions={0} | all-to-all | bytes 32768 | tf_op jit(solution)/shard_map/all_to_all | solution.py:57
  28.8 0.1 reshape.198
  28.9 16.5 %gather_fusion = f32[4096,128]{1,0:T(8,128)S(1)} fusion(f32[32768,128]{1,0:T(8,128)} %bitcast.64, s32[4096]{0:T(1024)S(1)} %broadcast_clamp_fusion), kind=kCustom, calls=%fused_computation | custom fusion | bytes 4210688 | tf_op jit(solution)/shard_map/jit(_take)/gather | solution.py:55
  45.5 0.0 copy-start.3
  45.5 0.0 copy-start.6
  45.5 0.0 copy-start.2
  45.5 2.4 %broadcast_select_fusion = f32[128,32,128]{2,1,0:T(8,128)} fusion(f32[128,32,128]{2,1,0:T(8,128)S(1)} %bitcast.65, pred[128,32]{1,0:T(8,128)(4,1)S(1)} %compare_and_fusion), kind=kLoop, calls=%fused_computation.15 | loop fusion | flops 524288 | bytes 4198400 | tf_op jit(solution)/shard_map/jit(_take)/select_n | solution.py:55
  48.0 4.8 %all-to-all-start.1 = ((f32[128,32,128]{2,1,0:T(8,128)}), f32[128,32,128]{2,1,0:T(8,128)S(1)}, u32[]{:S(2)}, u32[]{:S(2)}) async-start(f32[128,32,128]{2,1,0:T(8,128)} %broadcast_select_fusion), calls=%async_computation.1 | async-start | bytes 4194304 | tf_op jit(solution)/shard_map/all_to_all | solution.py:60
  52.8 0.1 reduce_sum.111
  52.8 0.0 copy-done.3
  52.9 0.1 reshape.192
  52.9 0.0 copy-done.6
  52.9 0.1 copy.25
  53.0 0.1 iota_compare_fusion.6
  53.2 0.0 copy-done
  53.2 0.0 copy-done.2
  53.2 0.4 fusion.38
  53.6 29.2 %all-to-all-done.1 = f32[128,32,128]{2,1,0:T(8,128)S(1)} async-done(((f32[128,32,128]{2,1,0:T(8,128)}), f32[128,32,128]{2,1,0:T(8,128)S(1)}, u32[]{:S(2)}, u32[]{:S(2)}) %all-to-all-start.1) | async-done | bytes 2097184 | tf_op jit(solution)/shard_map/all_to_all | solution.py:60
  82.8 0.0 copy-start.1
  82.8 0.0 copy-start.5
  82.8 15.3 %fusion.8 = f32[16,4,128]{2,1,0:T(4,128)S(1)} fusion(f32[4096,128,1,1]{1,0,3,2:T(8,128)S(1)} %bitcast.66, s32[16,4,32]{2,1,0:T(4,128)S(1)} %fusion.21, pred[16,4,32]{2,1,0:T(4,128)(4,1)S(1)} %iota_compare_fusion.6), kind=kOutput, calls=%fused_computation.9 | convolution fusion | flops 12893806592 | bytes 2140160 | tf_op jit(solution)/shard_map/dot_general | solution.py:65
  98.1 0.0 copy-start.4
  98.1 0.3 multiply_reduce_fusion
  98.5 0.0 copy-done.1
  98.5 0.0 copy-done.5
  98.5 0.9 fusion.12
  99.4 0.0 copy-done.4
  (6 shorter events, 0.2 us)
Async XLA Ops:
  0.6 52.5 %copy-start = (f32[128,1024]{1,0:T(8,128)S(1)}, f32[128,1024]{1,0:T(8,128)}, u32[]{:S(2)}) copy-start(f32[128,1024]{1,0:T(8,128)} %param.11) | copy-start | bytes 1572868
  45.5 7.4 %copy-start.3 = (s32[16,128]{1,0:T(8,128)S(1)}, s32[16,128]{1,0:T(8,128)}, u32[]{:S(2)}) copy-start(s32[16,128]{1,0:T(8,128)} %param.7) | copy-start | bytes 24580
  45.5 7.4 %copy-start.6 = (s32[16,4]{0,1:T(4,128)S(1)}, s32[16,4]{0,1:T(4,128)}, u32[]{:S(2)}) copy-start(s32[16,4]{0,1:T(4,128)} %param.8) | copy-start | bytes 772
  45.5 7.7 %copy-start.2 = (f32[16,128]{1,0:T(8,128)S(1)}, f32[16,128]{1,0:T(8,128)}, u32[]{:S(2)}) copy-start(f32[16,128]{1,0:T(8,128)} %param.10) | copy-start | bytes 24580
  48.0 34.8 %all-to-all-start.1 = ((f32[128,32,128]{2,1,0:T(8,128)}), f32[128,32,128]{2,1,0:T(8,128)S(1)}, u32[]{:S(2)}, u32[]{:S(2)}) async-start(f32[128,32,128]{2,1,0:T(8,128)} %broadcast_select_fusion), calls=%async_computation.1 | async-start | bytes 4194304 | tf_op jit(solution)/shard_map/all_to_all | solution.py:60
  82.8 15.7 %copy-start.1 = (f32[10,1024]{1,0:T(8,128)S(1)}, f32[10,1024]{1,0:T(8,128)}, u32[]{:S(2)}) copy-start(f32[10,1024]{1,0:T(8,128)} %param.12) | copy-start | bytes 122884
  82.8 15.7 %copy-start.5 = (f32[1024]{0:T(1024)S(1)}, f32[1024]{0:T(1024)}, u32[]{:S(2)}) copy-start(f32[1024]{0:T(1024)} %param.13) | copy-start | bytes 12292
  98.1 1.3 %copy-start.4 = (f32[16,4,128]{2,1,0:T(4,128)}, f32[16,4,128]{2,1,0:T(4,128)S(1)}, u32[]{:S(2)}) copy-start(f32[16,4,128]{2,1,0:T(4,128)S(1)} %fusion.8) | copy-start | bytes 98308
where the time goes:
time: 99.7 us; the launch traced here: 99.4 us
  waiting for transfers between devices  29.2 us (29%)
  blocking collectives  20.8 us (21%)
  matrix products  18.4 us (18%)
  local copies, waits for them, and re-layouts  17.1 us (17%)
  other arithmetic  8.24 us (8%)
  starting transfers between devices  4.79 us (5%)
    all_to_all x1, waiting for transfers between devices, shards(): lax.all_to_all(found, ('rows', 'cols'), split_axis=0, concat_axis=0, tile...  29.2 us
    all_to_all x1, blocking collectives, shards(): lax.all_to_all(outbox, ('rows', 'cols'), split_axis=0, concat_axis=0, til...  20.8 us
    gather x1, local copies, waits for them, and re-layouts, shards(): jnp.take(flat_table, lax.all_to_all(outbox, ('rows', 'cols'), split_axis=...  16.5 us
    dot_general x1, matrix products, shards(): jnp.dot(selector, fetched.reshape(devices * capacity, width), precision=l...  15.3 us
    all_to_all x1, starting transfers between devices, shards(): lax.all_to_all(found, ('rows', 'cols'), split_axis=0, concat_axis=0, tile...  4.79 us
    reduce_sum x1, other arithmetic, shards(): rank = jnp.sum(earlier.astype(jnp.int32), axis=1)  4.6 us
    select_n x2, other arithmetic, shards(): jnp.take(flat_table, lax.all_to_all(outbox, ('rows', 'cols'), split_axis=...  2.44 us
  transfers between devices with their start and end apart: 1, of which 1 were waited for; matrix products, arithmetic and copies ran while one was open for 1% of the time, Pallas kernels for 0%

commit v1 on v0

v1 whole, which is shorter than its diff:
```python
import jax
import jax.numpy as jnp
from jax import lax
from jax.experimental import pallas as pl
from jax.experimental.pallas import tpu as pltpu
from jax.sharding import PartitionSpec as P

NT = 4
L = 32
LANES = 128


def route_kernel(idx_ref, len_ref, code_ref, meta_ref, *, local_rows, devices, capacity):
    samples = idx_ref.shape[0]
    shift = local_rows.bit_length() - 1
    ids = idx_ref[...]
    target = ids >> shift
    lane = lax.broadcasted_iota(jnp.int32, (samples, LANES), 1)
    table = lane // L
    code = table * local_rows + (ids & (local_rows - 1))
    length = jnp.zeros((samples, LANES), jnp.int32)
    for t in range(NT):
        length = jnp.where(table == t, len_ref[:, t : t + 1], length)
    row = lax.broadcasted_iota(jnp.int32, (samples, LANES), 0)
    meta = jnp.where(lane - table * L < length, table * samples + row + 1, 0)
    high = (code >> 8).astype(jnp.float32)
    low = (code & 255).astype(jnp.float32)
    meta = meta.astype(jnp.float32)

    owner = lax.broadcasted_iota(jnp.int32, (devices, LANES), 0)
    hots = [
        jnp.where(owner == target[i : i + 1, :], 1.0, 0.0) for i in range(samples)
    ]
    earlier = lax.broadcasted_iota(jnp.int32, (LANES, 2 * LANES), 0)
    later = lax.broadcasted_iota(jnp.int32, (LANES, 2 * LANES), 1)
    counter = jnp.where(earlier < later, 1.0, 0.0).astype(jnp.bfloat16)
    hot_stack = jnp.concatenate(hots, axis=0).astype(jnp.bfloat16)
    counts = jnp.dot(hot_stack, counter, preferred_element_type=jnp.float32)
    place = lax.broadcasted_iota(jnp.int32, (capacity, LANES), 0).astype(jnp.float32)
    before = jnp.zeros((devices, LANES), jnp.float32)
    pieces = []
    for i in range(samples):
        block = counts[i * devices : (i + 1) * devices]
        rank = jnp.sum(hots[i] * (block[:, :LANES] + before), axis=0, keepdims=True)
        before = before + block[:, LANES:]
        here = place == rank
        pieces.append(
            jnp.concatenate(
                [
                    jnp.where(here, high[i : i + 1, :], 0.0),
                    jnp.where(here, low[i : i + 1, :], 0.0),
                    jnp.where(here, meta[i : i + 1, :], 0.0),
                ],
                axis=0,
            ).astype(jnp.bfloat16)
        )
    hot_wide = jnp.concatenate([h.astype(jnp.bfloat16) for h in hots], axis=1)
    values = jnp.concatenate(pieces, axis=1)
    box = lax.dot_general(
        hot_wide, values, (((1,), (1,)), ((), ())), preferred_element_type=jnp.float32
    )
    code_ref[...] = (
        box[:, :capacity] * 256.0 + box[:, capacity : 2 * capacity]
    ).astype(jnp.int32)
    meta_ref[...] = box[:, 2 * capacity :].astype(jnp.int32)


def gather_kernel(ids_ref, table_ref, out_ref, *, capacity):
    def one(src, carry):
        for c in range(capacity):
            out_ref[src * capacity + c, 0] = table_ref[ids_ref[src, c], 0]
        return carry

    lax.fori_loop(0, ids_ref.shape[0], one, 0)


def pool_kernel(rows_ref, meta_ref, dense_ref, base_ref, wpair_ref, pooled_ref, hidden_ref):
    groups = meta_ref.shape[0]
    samples = dense_ref.shape[0]
    bags = NT * samples
    bag = lax.broadcasted_iota(jnp.int32, (bags, LANES), 0) + 1
    total = jnp.zeros((bags, 2 * LANES), jnp.float32)
    rows = rows_ref[...]
    top = rows.astype(jnp.bfloat16)
    rest = (rows - top.astype(jnp.float32)).astype(jnp.bfloat16)
    select = jnp.concatenate(
        [jnp.where(meta_ref[g : g + 1, :] == bag, 1.0, 0.0) for g in range(groups)], axis=1
    ).astype(jnp.bfloat16)
    total = jnp.dot(
        select, jnp.concatenate([top, rest], axis=1), preferred_element_type=jnp.float32
    )
    pooled = total[:, :LANES] + total[:, LANES:]
    feats = [dense_ref[...]] + [pooled[t * samples : (t + 1) * samples] for t in range(NT)]
    for t in range(NT):
        pooled_ref[pl.ds(t, samples, stride=NT), :] = feats[t + 1]
    hidden = base_ref[...]
    k = 0
    for first in range(NT + 1):
        for second in range(first + 1, NT + 1):
            dots = jnp.sum(feats[first] * feats[second], axis=-1, keepdims=True)
            hidden = hidden + dots * wpair_ref[k : k + 1, :]
            k += 1
    hidden_ref[...] = jnp.maximum(hidden, 0.0)


def shards(bag_index, bag_length, emb_tables, dense_feats, w_dense, w_pair, top_bias):
    samples = bag_index.shape[0]
    local_rows = emb_tables.shape[1]
    width = emb_tables.shape[2]
    devices = lax.axis_size("rows") * lax.axis_size("cols")
    slots = samples * NT * L
    capacity = 2 * slots // devices
    units = w_dense.shape[1]
    places = devices * capacity

    import functools

    codes, meta = pl.pallas_call(
        functools.partial(
            route_kernel, local_rows=local_rows, devices=devices, capacity=capacity
        ),
        out_shape=(
            jax.ShapeDtypeStruct((devices, capacity), jnp.int32),
            jax.ShapeDtypeStruct((devices, capacity), jnp.int32),
        ),
        name="route",
    )(bag_index, bag_length)
    wanted = lax.all_to_all(codes, ("rows", "cols"), split_axis=0, concat_axis=0, tiled=True)
    found = pl.pallas_call(
        functools.partial(gather_kernel, capacity=capacity),
        out_shape=jax.ShapeDtypeStruct((places, 1, width), jnp.float32),
        in_specs=[
            pl.BlockSpec(memory_space=pltpu.SMEM),
            pl.BlockSpec(memory_space=pltpu.VMEM),
        ],
        out_specs=pl.BlockSpec(memory_space=pltpu.VMEM),
        compiler_params=pltpu.CompilerParams(vmem_limit_bytes=40 * 2**20),
        name="fetch",
    )(wanted, emb_tables.reshape(NT * local_rows, 1, width))
    fetched = lax.all_to_all(
        found.reshape(devices, capacity, width),
        ("rows", "cols"),
        split_axis=0,
        concat_axis=0,
        tiled=True,
    )
    base = jnp.dot(
        dense_feats, w_dense, precision=lax.Precision.HIGHEST, preferred_element_type=jnp.float32
    ) + top_bias
    pooled, hidden = pl.pallas_call(
        pool_kernel,
        out_shape=(
            jax.ShapeDtypeStruct((samples * NT, width), jnp.float32),
            jax.ShapeDtypeStruct((samples, units), jnp.float32),
        ),
        compiler_params=pltpu.CompilerParams(vmem_limit_bytes=24 * 2**20),
        name="pool",
    )(
        fetched.reshape(places, width),
        meta.reshape(places // LANES, LANES),
        dense_feats,
        base,
        w_pair,
    )
    return pooled.reshape(samples, NT, width), hidden


def solution(mesh):
    in_specs = (
        P(("rows", "cols"), None),
        P(("rows", "cols"), None),
        P(None, ("rows", "cols"), None),
        P(("rows", "cols"), None),
        P(),
        P(),
        P(),
    )
    out_specs = (P(("rows", "cols"), None, None), P(("rows", "cols"), None))
    return jax.shard_map(shards, mesh=mesh, in_specs=in_specs, out_specs=out_specs, check_vma=False)
```

time: 99.7 us -> 72.8 us (0.73)
  matrix products: 18.4 us -> 0.36 us
  local copies, waits for them, and re-layouts: 17.1 us -> 1.51 us
  Pallas kernels: 0 us -> 14.5 us
  other arithmetic: 8.24 us -> 0 us
    dot_general x4 -> x1, matrix products: 18.4 us -> 0.36 us  [shards(): jnp.dot(dense_feats, w_dense, precision=lax.Precision.HIGHEST, preferred_...]
    gather x1 -> x0, local copies, waits for them, and re-layouts: 16.5 us -> none  [shards(): jnp.take(flat_table, lax.all_to_all(outbox, ('rows', 'cols'), split_axis=...]
    pallas_call x0 -> x3, Pallas kernels: none -> 14.5 us  [the longest x1 11 us: shards(): pl.pallas_call(functools.partial(gather_kernel, capacity=capacity), out_s...]
    reduce_sum x2 -> x0, other arithmetic: 4.86 us -> none  [the longest x1 4.6 us: shards(): rank = jnp.sum(earlier.astype(jnp.int32), axis=1)]
    select_n x2 -> x0, other arithmetic: 2.44 us -> none  [shards(): jnp.take(flat_table, lax.all_to_all(outbox, ('rows', 'cols'), split_axis=...]
    unnamed x15 -> x11, local copies, waits for them, and re-layouts: 0.12 us -> 1.44 us
where the time goes in v1:
time: 72.8 us; the launch traced here: 72.4 us
  waiting for transfers between devices  29.7 us (41%)
  blocking collectives  20.9 us (29%)
  Pallas kernels  14.5 us (20%)
  starting transfers between devices  4.62 us (6%)
  local copies, waits for them, and re-layouts  1.51 us (2%)
    all_to_all x1, waiting for transfers between devices, shards(): lax.all_to_all(found.reshape(devices, capacity, width), ('rows', 'cols'),...  29.7 us
    all_to_all x1, blocking collectives, shards(): lax.all_to_all(codes, ('rows', 'cols'), split_axis=0, concat_axis=0, tile...  20.9 us
    pallas_call x1, Pallas kernels, shards(): pl.pallas_call(functools.partial(gather_kernel, capacity=capacity), out_s...  11 us
    all_to_all x1, starting transfers between devices, shards(): lax.all_to_all(found.reshape(devices, capacity, width), ('rows', 'cols'),...  4.62 us
    pallas_call x1, Pallas kernels, shards(): pl.pallas_call(functools.partial(route_kernel, local_rows=local_rows, dev...  2.25 us
  transfers between devices with their start and end apart: 1, of which 1 were waited for; matrix products, arithmetic and copies ran while one was open for 1% of the time, Pallas kernels for 0%

profile of v1, /device:TPU:1, one launch (start us, length us, event | category | flops | bytes accessed | tf_op | source)
XLA Modules:
  0.0 72.4 jit_solution(12147543806044214582)
XLA Ops:
  0.6 0.0 copy-start
  0.6 1.4 %copy.11.len_ref = s32[16,4]{1,0:T(8,128)} copy(s32[16,4]{0,1:T(4,128)} %param.8) | data formatting | bytes 512 | tf_op args[1]
  2.1 2.3 %route.1 = (s32[128,32]{1,0:T(8,128)}, s32[128,32]{1,0:T(8,128)}) custom-call(s32[16,128]{1,0:T(8,128)} %idx_ref.1, s32[16,4]{1,0:T(8,128)} %copy.11.len_ref), custom_call_target="tpu_custom_call" | custom-call | tf_op jit(solution)/shard_map/route/pallas_call | solution.py:118
  4.3 20.9 %all_to_all.16 = s32[128,1,32]{2,1,0:T(1,128)S(1)} all-to-all(s32[128,1,32]{2,1,0:T(1,128)} %bitcast.13), channel_id=1, replica_groups=mesh['rows'=16,'cols'=8] {'rows','cols'}, dimensions={0} | all-to-all | bytes 32768 | tf_op jit(solution)/shard_map/all_to_all | solution.py:128
  25.3 11.0 %fetch.1 = f32[4096,1,128]{2,1,0:T(1,128)} custom-call(s32[128,32]{1,0:T(8,128)S(1)} %bitcast.11, f32[32768,1,128]{2,1,0:T(1,128)} %bitcast.12), custom_call_target="tpu_custom_call" | custom-call | tf_op jit(solution)/shard_map/fetch/pallas_call | solution.py:129
  36.3 0.0 copy-start.3
  36.3 0.0 copy-start.2
  36.3 0.0 copy-start.4
  36.3 0.0 copy-start.1
  36.3 4.6 %all-to-all-start.1 = ((f32[128,32,128]{2,1,0:T(8,128)}), f32[128,32,128]{2,1,0:T(8,128)S(1)}, u32[]{:S(2)}, u32[]{:S(2)}) async-start(f32[128,32,128]{2,1,0:T(8,128)} %bitcast.4), calls=%async_computation.1 | async-start | bytes 4194304 | tf_op jit(solution)/shard_map/all_to_all | solution.py:140
  40.9 0.0 copy-done.3
  40.9 0.1 reshape.25.meta_ref
  41.0 0.0 copy-done
  41.0 0.0 copy-done.2
  41.0 0.0 copy-done.4
  41.0 0.4 convolution_add_fusion.base_ref
  41.4 29.7 %all-to-all-done.1 = f32[128,32,128]{2,1,0:T(8,128)S(1)} async-done(((f32[128,32,128]{2,1,0:T(8,128)}), f32[128,32,128]{2,1,0:T(8,128)S(1)}, u32[]{:S(2)}, u32[]{:S(2)}) %all-to-all-start.1) | async-done | bytes 2097184 | tf_op jit(solution)/shard_map/all_to_all | solution.py:140
  71.1 0.0 copy-done.1
  71.1 1.2 %pool.1 = (f32[64,128]{1,0:T(8,128)}, f32[16,1024]{1,0:T(8,128)}) custom-call(f32[4096,128]{1,0:T(8,128)S(1)} %bitcast.10, s32[32,128]{1,0:T(8,128)S(1)} %reshape.25.meta_ref, f32[16,128]{1,0:T(8,128)S(1)} %copy-done.2, f32[16,1024]{1,0:T(8,128)S(1)} %convolution_add_fusion.base_ref, f32[10,1024]{1,0:T(8,128)S(1)} %copy-done.1), custom_call_target="tpu_custom_call" | custom-call | tf_op jit(solution)/shard_map/pool/pallas_call | solution.py:150
Async XLA Ops:
  0.6 40.4 %copy-start = (f32[128,1024]{1,0:T(8,128)S(1)}, f32[128,1024]{1,0:T(8,128)}, u32[]{:S(2)}) copy-start(f32[128,1024]{1,0:T(8,128)} %param.11) | copy-start | bytes 1572868
  36.3 4.6 %copy-start.3 = (s32[128,32]{1,0:T(8,128)S(1)}, s32[128,32]{1,0:T(8,128)}, u32[]{:S(2)}) copy-start(s32[128,32]{1,0:T(8,128)} %get-tuple-element.7) | copy-start | bytes 49156
  36.3 4.7 %copy-start.2 = (f32[16,128]{1,0:T(8,128)S(1)}, f32[16,128]{1,0:T(8,128)}, u32[]{:S(2)}) copy-start(f32[16,128]{1,0:T(8,128)} %dense_ref.1) | copy-start | bytes 24580
  36.3 4.7 %copy-start.4 = (f32[1024]{0:T(1024)S(1)}, f32[1024]{0:T(1024)}, u32[]{:S(2)}) copy-start(f32[1024]{0:T(1024)} %param.13) | copy-start | bytes 12292
  36.3 34.8 %copy-start.1 = (f32[10,1024]{1,0:T(8,128)S(1)}, f32[10,1024]{1,0:T(8,128)}, u32[]{:S(2)}) copy-start(f32[10,1024]{1,0:T(8,128)} %wpair_ref.1) | copy-start | bytes 122884
  36.3 34.8 %all-to-all-start.1 = ((f32[128,32,128]{2,1,0:T(8,128)}), f32[128,32,128]{2,1,0:T(8,128)S(1)}, u32[]{:S(2)}, u32[]{:S(2)}) async-start(f32[128,32,128]{2,1,0:T(8,128)} %bitcast.4), calls=%async_computation.1 | async-start | bytes 4194304 | tf_op jit(solution)/shard_map/all_to_all | solution.py:140

commit v2 on v1

v2 whole, which is shorter than its diff:
```python
import functools

import jax
import jax.numpy as jnp
from jax import lax
from jax.experimental import pallas as pl
from jax.experimental.pallas import tpu as pltpu
from jax.sharding import PartitionSpec as P

NT = 4
L = 32
LANES = 128
BOTH_LANES = (((1,), (1,)), ((), ()))


def iota(shape, axis):
    return lax.broadcasted_iota(jnp.int32, shape, axis)


def route_kernel(idx_ref, code_ref, rank_ref, *, local_rows, devices, capacity):
    samples = idx_ref.shape[0]
    ids = idx_ref[...]
    target = ids >> (local_rows.bit_length() - 1)
    code = iota((samples, LANES), 1) // L * local_rows + (ids & (local_rows - 1))
    high = (code >> 8).astype(jnp.float32)
    low = (code & 255).astype(jnp.float32)

    owner = iota((devices, LANES), 0)
    hots = [jnp.where(owner == target[i : i + 1, :], 1.0, 0.0) for i in range(samples)]
    hot_stack = jnp.concatenate(hots, axis=0).astype(jnp.bfloat16)
    counter = jnp.where(
        iota((LANES, 2 * LANES), 0) < iota((LANES, 2 * LANES), 1), 1.0, 0.0
    ).astype(jnp.bfloat16)
    counts = jnp.dot(hot_stack, counter, preferred_element_type=jnp.float32)
    place = iota((capacity, LANES), 0).astype(jnp.float32)
    before = jnp.zeros((devices, LANES), jnp.float32)
    pieces = []
    for i in range(samples):
        block = counts[i * devices : (i + 1) * devices]
        rank = jnp.sum(hots[i] * (block[:, :LANES] + before), axis=0, keepdims=True)
        rank_ref[i : i + 1, :] = rank
        before = before + block[:, LANES:]
        here = place == rank
        pieces.append(
            jnp.concatenate(
                [
                    jnp.where(here, high[i : i + 1, :], 0.0),
                    jnp.where(here, low[i : i + 1, :], 0.0),
                ],
                axis=0,
            ).astype(jnp.bfloat16)
        )
    hot_wide = jnp.concatenate([h.astype(jnp.bfloat16) for h in hots], axis=1)
    values = jnp.concatenate(pieces, axis=1)
    box = lax.dot_general(hot_wide, values, BOTH_LANES, preferred_element_type=jnp.float32)
    code_ref[...] = (box[:, :capacity] * 256.0 + box[:, capacity:]).astype(jnp.int32)


def fetch_kernel(
    wanted_ref, idx_ref, rank_ref, len_ref, dense_ref, wdense_ref, bias_ref, table_ref,
    out_ref, select_ref, base_ref, ids_ref, sem,
    *, local_rows, capacity,
):
    copy = pltpu.make_async_copy(wanted_ref, ids_ref, sem)
    copy.start()
    samples = idx_ref.shape[0]
    target = idx_ref[...] >> (local_rows.bit_length() - 1)
    per_row = LANES // capacity
    groups = select_ref.shape[1] // LANES
    group = target // per_row
    key = (target - group * per_row) * capacity + rank_ref[...].astype(jnp.int32)
    spread = jnp.where(iota((NT, LANES), 1) // L == iota((NT, LANES), 0), 1.0, 0.0)
    length = lax.dot_general(
        len_ref[...].astype(jnp.float32).astype(jnp.bfloat16),
        spread.astype(jnp.bfloat16),
        (((0,), (0,)), ((), ())),
        preferred_element_type=jnp.float32,
    ).astype(jnp.int32)
    lane = iota((samples, LANES), 1)
    bag = lane // L * samples + iota((samples, LANES), 0) + 1
    bag = jnp.where(lane % L < length, bag, 0).astype(jnp.float32)
    left, right = [], []
    for i in range(samples):
        left.append(jnp.where(iota((groups, LANES), 0) == group[i : i + 1, :], 1.0, 0.0))
        right.append(
            jnp.where(iota((LANES, LANES), 0) == key[i : i + 1, :], bag[i : i + 1, :], 0.0)
        )
    bags = lax.dot_general(
        jnp.concatenate(left, axis=1).astype(jnp.bfloat16),
        jnp.concatenate(right, axis=1).astype(jnp.bfloat16),
        BOTH_LANES,
        preferred_element_type=jnp.float32,
    ).astype(jnp.int32)
    own = iota((NT * samples, LANES), 0) + 1
    for g in range(groups):
        select_ref[:, g * LANES : (g + 1) * LANES] = jnp.where(
            bags[g : g + 1, :] == own, 1.0, 0.0
        ).astype(jnp.bfloat16)
    base_ref[...] = (
        jnp.dot(
            dense_ref[...],
            wdense_ref[...],
            precision=lax.Precision.HIGHEST,
            preferred_element_type=jnp.float32,
        )
        + bias_ref[...]
    )
    copy.wait()

    def one(src, carry):
        for c in range(capacity):
            out_ref[src * capacity + c, 0] = table_ref[ids_ref[src, c], 0]
        return carry

    for src in range(ids_ref.shape[0]):
        one(src, 0)


def pool_kernel(rows_ref, select_ref, dense_ref, base_ref, wpair_ref, pooled_ref, hidden_ref):
    samples = dense_ref.shape[0]
    rows = rows_ref[...]
    top = rows.astype(jnp.bfloat16)
    rest = (rows - top.astype(jnp.float32)).astype(jnp.bfloat16)
    total = jnp.dot(
        select_ref[...],
        jnp.concatenate([top, rest], axis=1),
        preferred_element_type=jnp.float32,
    )
    pooled = total[:, :LANES] + total[:, LANES:]
    feats = [dense_ref[...]] + [pooled[t * samples : (t + 1) * samples] for t in range(NT)]
    for t in range(NT):
        pooled_ref[pl.ds(t, samples, stride=NT), :] = feats[t + 1]
    hidden = base_ref[...]
    k = 0
    for first in range(NT + 1):
        for second in range(first + 1, NT + 1):
            dots = jnp.sum(feats[first] * feats[second], axis=-1, keepdims=True)
            hidden = hidden + dots * wpair_ref[k : k + 1, :]
            k += 1
    hidden_ref[...] = jnp.maximum(hidden, 0.0)


def shards(bag_index, bag_length, emb_tables, dense_feats, w_dense, w_pair, top_bias):
    samples = bag_index.shape[0]
    local_rows = emb_tables.shape[1]
    width = emb_tables.shape[2]
    devices = lax.axis_size("rows") * lax.axis_size("cols")
    slots = samples * NT * L
    capacity = 2 * slots // devices
    units = w_dense.shape[1]
    places = devices * capacity
    vmem = pl.BlockSpec(memory_space=pltpu.VMEM)

    codes, rank = pl.pallas_call(
        functools.partial(
            route_kernel, local_rows=local_rows, devices=devices, capacity=capacity
        ),
        out_shape=(
            jax.ShapeDtypeStruct((devices, capacity), jnp.int32),
            pltpu.VMEM((samples, LANES), jnp.float32),
        ),
        compiler_params=pltpu.CompilerParams(vmem_limit_bytes=8 * 2**20),
        cost_estimate=pl.CostEstimate(flops=10**10, bytes_accessed=10**8, transcendentals=0),
        name="route",
    )(bag_index)
    wanted = lax.all_to_all(codes, ("rows", "cols"), split_axis=0, concat_axis=0, tiled=True)
    found, select, base = pl.pallas_call(
        functools.partial(fetch_kernel, local_rows=local_rows, capacity=capacity),
        out_shape=(
            pltpu.VMEM((places, 1, width), jnp.float32),
            pltpu.VMEM((samples * NT, places), jnp.bfloat16),
            pltpu.VMEM((samples, units), jnp.float32),
        ),
        in_specs=[vmem] * 8,
        out_specs=(vmem, vmem, vmem),
        scratch_shapes=[pltpu.SMEM((devices, capacity), jnp.int32), pltpu.SemaphoreType.DMA],
        compiler_params=pltpu.CompilerParams(vmem_limit_bytes=8 * 2**20),
        name="fetch",
    )(
        wanted,
        bag_index,
        rank,
        bag_length.T,
        dense_feats,
        w_dense,
        top_bias.reshape(1, units),
        emb_tables.reshape(NT * local_rows, 1, width),
    )
    fetched = lax.all_to_all(
        found.reshape(devices, capacity, width),
        ("rows", "cols"),
        split_axis=0,
        concat_axis=0,
        tiled=True,
    )
    pooled, hidden = pl.pallas_call(
        pool_kernel,
        out_shape=(
            jax.ShapeDtypeStruct((samples * NT, width), jnp.float32),
            jax.ShapeDtypeStruct((samples, units), jnp.float32),
        ),
        compiler_params=pltpu.CompilerParams(vmem_limit_bytes=16 * 2**20),
        name="pool",
    )(fetched.reshape(places, width), select, dense_feats, base, w_pair)
    return pooled.reshape(samples, NT, width), hidden


def solution(mesh):
    in_specs = (
        P(("rows", "cols"), None),
        P(("rows", "cols"), None),
        P(None, ("rows", "cols"), None),
        P(("rows", "cols"), None),
        P(),
        P(),
        P(),
    )
    out_specs = (P(("rows", "cols"), None, None), P(("rows", "cols"), None))
    return jax.shard_map(shards, mesh=mesh, in_specs=in_specs, out_specs=out_specs, check_vma=False)
```

time: 72.8 us -> 63 us (0.87)
  blocking collectives: 20.9 us -> 55.4 us
  waiting for transfers between devices: 29.7 us -> 0 us
  Pallas kernels: 14.5 us -> 5.91 us
  starting transfers between devices: 4.62 us -> 0 us
  local copies, waits for them, and re-layouts: 1.51 us -> 0.78 us
    all_to_all x0 -> x1, blocking collectives: none -> 34.6 us  [shards(): lax.all_to_all(found.reshape(devices, capacity, width), ('rows', 'cols'),...]
    all_to_all x1 -> x0, waiting for transfers between devices: 29.7 us -> none  [shards(): lax.all_to_all(found.reshape(devices, capacity, width), ('rows', 'cols'),...]
    pallas_call x1, Pallas kernels: 11 us -> 3.78 us  [shards(): pl.pallas_call(functools.partial(fetch_kernel, local_rows=local_rows, cap...]
    all_to_all x1 -> x0, starting transfers between devices: 4.62 us -> none  [shards(): lax.all_to_all(found.reshape(devices, capacity, width), ('rows', 'cols'),...]
    pallas_call x1, Pallas kernels: 2.25 us -> 0.88 us  [shards(): pl.pallas_call(functools.partial(route_kernel, local_rows=local_rows, dev...]
  transfers between devices with their start and end apart: 1 -> 0, of which waited for: 1 -> 0; matrix products, arithmetic and copies ran while one was open for 1% -> 0% of each run, Pallas kernels for 0% -> 0%
where the time goes in v2:
time: 63 us; the launch traced here: 62.8 us
  blocking collectives  55.4 us (88%)
  Pallas kernels  5.91 us (9%)
  local copies, waits for them, and re-layouts  0.78 us (1%)
  between operations  0.71 us (1%)
    all_to_all x1, blocking collectives, shards(): lax.all_to_all(found.reshape(devices, capacity, width), ('rows', 'cols'),...  34.6 us
    all_to_all x1, blocking collectives, shards(): lax.all_to_all(codes, ('rows', 'cols'), split_axis=0, concat_axis=0, tile...  20.8 us
    pallas_call x1, Pallas kernels, shards(): pl.pallas_call(functools.partial(fetch_kernel, local_rows=local_rows, cap...  3.78 us

profile of v2, /device:TPU:1, one launch (start us, length us, event | category | flops | bytes accessed | tf_op | source)
XLA Modules:
  0.0 62.8 jit_solution(1917747467263530724)
XLA Ops:
  0.6 0.0 copy-start.3
  0.6 0.0 copy-start.1
  0.7 0.0 copy-start.4
  0.7 0.7 %copy-done.4 = s32[16,128]{1,0:T(8,128)S(1)} copy-done((s32[16,128]{1,0:T(8,128)S(1)}, s32[16,128]{1,0:T(8,128)}, u32[]{:S(2)}) %copy-start.4) | copy-done | bytes 8216
  1.4 0.0 copy-start
  1.4 0.0 copy-start.5
  1.4 0.0 copy-start.6
  1.4 0.0 copy-start.7
  1.4 0.9 %route.1 = (s32[128,32]{1,0:T(8,128)S(1)}, f32[16,128]{1,0:T(8,128)S(1)}) custom-call(s32[16,128]{1,0:T(8,128)S(1)} %copy-done.4), custom_call_target="tpu_custom_call" | custom-call | flops 10000000000 | bytes 100000000 | tf_op jit(solution)/shard_map/route/pallas_call | solution.py:154
  2.3 20.8 %all_to_all.16 = s32[128,1,32]{2,1,0:T(1,128)S(1)} all-to-all(s32[128,1,32]{2,1,0:T(1,128)S(1)} %bitcast.14), channel_id=1, replica_groups=mesh['rows'=16,'cols'=8] {'rows','cols'}, dimensions={0} | all-to-all | bytes 32768 | tf_op jit(solution)/shard_map/all_to_all | solution.py:166
  23.1 0.0 copy-done.3
  23.1 0.0 copy-done.1
  23.1 0.0 copy-done
  23.1 0.0 copy-done.5
  23.1 0.0 copy-done.6
  23.2 0.0 copy-done.7
  23.2 3.8 %fetch.1 = (f32[4096,1,128]{2,1,0:T(1,128)S(1)}, bf16[64,4096]{1,0:T(8,128)(2,1)S(1)}, f32[16,1024]{1,0:T(8,128)S(1)}) custom-call(s32[128,32]{1,0:T(8,128)S(1)} %bitcast.13, s32[16,128]{1,0:T(8,128)S(1)} %copy-done.5, f32[16,128]{1,0:T(8,128)S(1)} %get-tuple-element.10.rank_ref, s32[4,16]{1,0:T(4,128)S(1)} %bitcast.16, f32[16,128]{1,0:T(8,128)S(1)} %copy-done.3, ...), custom_call_target="tpu_custom_call" | custom-call | tf_op jit(solution)/shard_map/fetch/pallas_call | solution.py:167
  27.0 0.0 copy-start.2
  27.0 34.6 %all_to_all.17 = f32[128,32,128]{2,1,0:T(8,128)S(1)} all-to-all(f32[128,32,128]{2,1,0:T(8,128)S(1)} %bitcast.12), channel_id=1, replica_groups=mesh['rows'=16,'cols'=8] {'rows','cols'}, dimensions={0} | all-to-all | bytes 4194304 | tf_op jit(solution)/shard_map/all_to_all | solution.py:189
  61.6 0.0 copy-done.2
  61.6 1.2 %pool.1 = (f32[64,128]{1,0:T(8,128)}, f32[16,1024]{1,0:T(8,128)}) custom-call(f32[4096,128]{1,0:T(8,128)S(1)} %bitcast.11, bf16[64,4096]{1,0:T(8,128)(2,1)S(1)} %get-tuple-element.12.select_ref, f32[16,128]{1,0:T(8,128)S(1)} %copy-done.3, f32[16,1024]{1,0:T(8,128)S(1)} %get-tuple-element.13.base_ref, f32[10,1024]{1,0:T(8,128)S(1)} %copy-done.2), custom_call_target="tpu_custom_call" | custom-call | tf_op jit(solution)/shard_map/pool/pallas_call | solution.py:196
Async XLA Ops:
  0.6 22.5 %copy-start.3 = (f32[16,128]{1,0:T(8,128)S(1)}, f32[16,128]{1,0:T(8,128)}, u32[]{:S(2)}) copy-start(f32[16,128]{1,0:T(8,128)} %dense_ref.3) | copy-start | bytes 24580
  0.6 22.5 %copy-start.1 = (f32[128,1024]{1,0:T(8,128)S(1)}, f32[128,1024]{1,0:T(8,128)}, u32[]{:S(2)}) copy-start(f32[128,1024]{1,0:T(8,128)} %wdense_ref.1) | copy-start | bytes 1572868
  0.7 0.8 %copy-start.4 = (s32[16,128]{1,0:T(8,128)S(1)}, s32[16,128]{1,0:T(8,128)}, u32[]{:S(2)}) copy-start(s32[16,128]{1,0:T(8,128)} %idx_ref.3) | copy-start | bytes 24580
  1.4 21.7 %copy-start = (f32[4,8192,128]{2,1,0:T(8,128)S(1)}, f32[4,8192,128]{2,1,0:T(8,128)}, u32[]{:S(2)}) copy-start(f32[4,8192,128]{2,1,0:T(8,128)} %param.9) | copy-start | bytes 50331652
  1.4 21.7 %copy-start.5 = (s32[16,128]{1,0:T(8,128)S(1)}, s32[16,128]{1,0:T(8,128)}, u32[]{:S(2)}) copy-start(s32[16,128]{1,0:T(8,128)} %idx_ref.3) | copy-start | bytes 24580
  1.4 21.7 %copy-start.6 = (f32[1024]{0:T(1024)S(1)}, f32[1024]{0:T(1024)}, u32[]{:S(2)}) copy-start(f32[1024]{0:T(1024)} %param.13) | copy-start | bytes 12292
  1.4 21.7 %copy-start.7 = (s32[16,4]{0,1:T(4,128)S(1)}, s32[16,4]{0,1:T(4,128)}, u32[]{:S(2)}) copy-start(s32[16,4]{0,1:T(4,128)} %param.8) | copy-start | bytes 772
  27.0 34.6 %copy-start.2 = (f32[10,1024]{1,0:T(8,128)S(1)}, f32[10,1024]{1,0:T(8,128)}, u32[]{:S(2)}) copy-start(f32[10,1024]{1,0:T(8,128)} %wpair_ref.1) | copy-start | bytes 122884

commit v3 on v2

v3 whole, which is shorter than its diff:
```python
import functools

import jax
import jax.numpy as jnp
from jax import lax
from jax.experimental import pallas as pl
from jax.experimental.pallas import tpu as pltpu
from jax.sharding import PartitionSpec as P

NT = 4
L = 32
LANES = 128
SMALL = 26
BOTH_LANES = (((1,), (1,)), ((), ()))


def iota(shape, axis):
    return lax.broadcasted_iota(jnp.int32, shape, axis)


def ones_where(mask):
    return jnp.where(mask, 1.0, 0.0)


def route_kernel(idx_ref, len_ref, message_ref, place_ref, *, local_rows, devices, capacity, small):
    samples = idx_ref.shape[0]
    ids = idx_ref[...]
    lane = iota((samples, LANES), 1)
    spread = ones_where(iota((NT, LANES), 1) // L == iota((NT, LANES), 0)).astype(jnp.bfloat16)
    length = lax.dot_general(
        len_ref[...].astype(jnp.float32).astype(jnp.bfloat16),
        spread,
        (((0,), (0,)), ((), ())),
        preferred_element_type=jnp.float32,
    ).astype(jnp.int32)
    target = jnp.where(lane % L < length, ids >> (local_rows.bit_length() - 1), -1)
    code = lane // L * local_rows + (ids & (local_rows - 1))
    high = (code & -256).astype(jnp.float32)
    low = (code & 255).astype(jnp.float32)

    owner = iota((devices, LANES), 0)
    hots = [ones_where(owner == target[i : i + 1, :]) for i in range(samples)]
    row = iota((LANES, LANES), 0)
    column = iota((LANES, LANES), 1)
    ones = jnp.ones((LANES, LANES), jnp.float32)
    counter = jnp.concatenate(
        [
            ones_where(row < column),
            ones,
            ones_where((row < column) & (row // L == column // L)),
        ],
        axis=1,
    ).astype(jnp.bfloat16)
    counts = jnp.dot(
        jnp.concatenate(hots, axis=0).astype(jnp.bfloat16),
        counter,
        preferred_element_type=jnp.float32,
    )
    firsts = [
        jnp.where(counts[i * devices : (i + 1) * devices, 2 * LANES :] == 0.0, hots[i], 0.0)
        for i in range(samples)
    ]
    groups = jnp.dot(
        jnp.concatenate(firsts, axis=0).astype(jnp.bfloat16),
        jnp.concatenate([ones_where(row <= column), ones], axis=1).astype(jnp.bfloat16),
        preferred_element_type=jnp.float32,
    )
    slot = iota((capacity, LANES), 0).astype(jnp.float32)
    before = jnp.zeros((devices, LANES), jnp.float32)
    groups_before = jnp.zeros((devices, LANES), jnp.float32)
    uppers, lowers = [], []
    for i in range(samples):
        block = counts[i * devices : (i + 1) * devices]
        group = groups[i * devices : (i + 1) * devices]
        rank = jnp.sum(hots[i] * (block[:, :LANES] + before), axis=0, keepdims=True)
        which = jnp.sum(hots[i] * (group[:, :LANES] + groups_before), axis=0, keepdims=True)
        first = jnp.sum(firsts[i], axis=0, keepdims=True)
        before = before + block[:, LANES : 2 * LANES]
        groups_before = groups_before + group[:, LANES:]
        here = slot == rank
        uppers.append(
            jnp.concatenate(
                [jnp.where(here, high[i : i + 1, :], 0.0), jnp.where(here, which, 0.0)], axis=0
            ).astype(jnp.bfloat16)
        )
        lowers.append(jnp.where(here, low[i : i + 1, :], 0.0).astype(jnp.bfloat16))
        own = target[i : i + 1, :] * small + which.astype(jnp.int32) - 1
        place_ref[i : i + 1, :] = jnp.where((first > 0.0) & (which <= small), own, -1)
    hot_wide = jnp.concatenate([h.astype(jnp.bfloat16) for h in hots], axis=1)
    slots = samples * LANES
    upper = jnp.concatenate(
        [jnp.concatenate(uppers, axis=1), jnp.zeros((LANES - 2 * capacity, slots), jnp.bfloat16)],
        axis=0,
    )
    lower = jnp.concatenate(
        [jnp.concatenate(lowers, axis=1), jnp.zeros((LANES - capacity, slots), jnp.bfloat16)],
        axis=0,
    )
    box = lax.dot_general(
        hot_wide, upper, BOTH_LANES, preferred_element_type=jnp.float32
    ) + lax.dot_general(hot_wide, lower, BOTH_LANES, preferred_element_type=jnp.float32)
    need = jnp.max(groups_before, axis=0, keepdims=True)
    message_ref[...] = jnp.where(
        iota((devices, LANES), 1) < 2 * capacity, box, need
    ).astype(jnp.int32)


def fetch_kernel(
    wanted_ref, place_ref, dense_ref, wdense_ref, bias_ref, table_ref,
    out_ref, select_ref, base_ref, need_ref, ids_ref, key_ref, rows_ref, sem,
    *, capacity, small, rolled,
):
    copy = pltpu.make_async_copy(wanted_ref, ids_ref, sem)
    copy.start()
    devices = wanted_ref.shape[0]
    samples = place_ref.shape[0]
    per_block = LANES // capacity
    blocks = devices // per_block
    rows_out = per_block * small

    wanted = wanted_ref[...]
    need = jnp.max(
        jnp.where(iota((devices, LANES), 1) < 2 * capacity, 0, wanted), axis=0, keepdims=True
    )
    need_ref[...] = jnp.broadcast_to(need, need_ref.shape)
    keys = jnp.zeros((blocks, LANES), jnp.int32)
    for k in range(per_block):
        which = wanted_ref[pl.ds(k, blocks, stride=per_block), :]
        which = pltpu.roll(which, (k - 1) * capacity % LANES, axis=1)
        which = jnp.where((which > 0) & (which <= small), which + (k * small - 1), -1)
        keys = jnp.where(iota((blocks, LANES), 1) // capacity == k, which, keys)
    for b in range(blocks):
        key_ref[b] = keys[b : b + 1, :]

    place = place_ref[...]
    parts = select_ref.shape[1] // LANES
    padded = -(-parts // 8) * 8
    part = place >> 7
    spot = place & (LANES - 1)
    lane = iota((1, LANES), 1)
    left, right = [], []
    for i in range(samples):
        bag = (lane // L * samples + (i + 1)).astype(jnp.float32)
        left.append(ones_where(iota((padded, LANES), 0) == part[i : i + 1, :]))
        right.append(jnp.where(iota((LANES, LANES), 0) == spot[i : i + 1, :], bag, 0.0))
    bags = lax.dot_general(
        jnp.concatenate(left, axis=1).astype(jnp.bfloat16),
        jnp.concatenate(right, axis=1).astype(jnp.bfloat16),
        BOTH_LANES,
        preferred_element_type=jnp.float32,
    ).astype(jnp.int32)
    own = iota((NT * samples, LANES), 0) + 1
    for g in range(parts):
        select_ref[:, g * LANES : (g + 1) * LANES] = ones_where(bags[g : g + 1, :] == own).astype(
            jnp.bfloat16
        )
    base_ref[...] = (
        jnp.dot(
            dense_ref[...],
            wdense_ref[...],
            precision=lax.Precision.HIGHEST,
            preferred_element_type=jnp.float32,
        )
        + bias_ref[...]
    )
    copy.wait()

    def one(b, hold):
        for k in range(per_block):
            for c in range(capacity):
                at = hold + k * capacity + c
                rows_ref[at : at + 1, :] = table_ref[ids_ref[b * per_block + k, c]]
        rows = rows_ref[hold : hold + LANES, :]
        top = rows.astype(jnp.bfloat16)
        rest = (rows - top.astype(jnp.float32)).astype(jnp.bfloat16)
        gather = ones_where(iota((rows_out, LANES), 0) == key_ref[b]).astype(jnp.bfloat16)
        sums = jnp.dot(
            gather, jnp.concatenate([top, rest], axis=1), preferred_element_type=jnp.float32
        )
        start = b * rows_out if isinstance(b, int) else pl.multiple_of(b * rows_out, 8)
        out_ref[pl.ds(start, rows_out), :] = sums[:, :LANES] + sums[:, LANES:]

    if rolled:
        lax.fori_loop(0, blocks, lambda b, carry: (one(b, 0), carry)[1], 0)
    else:
        for b in range(blocks):
            one(b, b * LANES)


def pool_kernel(
    rows_ref, select_ref, dense_ref, base_ref, wpair_ref, need_ref,
    pooled_ref, hidden_ref, over_ref,
    *, small,
):
    over_ref[0] = (jnp.max(need_ref[...]) > small).astype(jnp.int32)
    samples = dense_ref.shape[0]
    rows = rows_ref[...]
    top = rows.astype(jnp.bfloat16)
    rest = (rows - top.astype(jnp.float32)).astype(jnp.bfloat16)
    total = jnp.dot(
        select_ref[...],
        jnp.concatenate([top, rest], axis=1),
        preferred_element_type=jnp.float32,
    )
    pooled = total[:, :LANES] + total[:, LANES:]
    feats = [dense_ref[...]] + [pooled[t * samples : (t + 1) * samples] for t in range(NT)]
    for t in range(NT):
        pooled_ref[pl.ds(t, samples, stride=NT), :] = feats[t + 1]
    hidden = base_ref[...]
    k = 0
    for first in range(NT + 1):
        for second in range(first + 1, NT + 1):
            dots = jnp.sum(feats[first] * feats[second], axis=-1, keepdims=True)
            hidden = hidden + dots * wpair_ref[k : k + 1, :]
            k += 1
    hidden_ref[...] = jnp.maximum(hidden, 0.0)


def exchange(
    bag_index, bag_length, emb_tables, dense_feats, w_dense, w_pair, top_bias, *, small, rolled
):
    samples = bag_index.shape[0]
    local_rows = emb_tables.shape[1]
    width = emb_tables.shape[2]
    devices = lax.axis_size("rows") * lax.axis_size("cols")
    capacity = 2 * samples * NT * L // devices
    units = w_dense.shape[1]
    places = devices * small
    vmem = pl.BlockSpec(memory_space=pltpu.VMEM)

    message, place = pl.pallas_call(
        functools.partial(
            route_kernel, local_rows=local_rows, devices=devices, capacity=capacity, small=small
        ),
        out_shape=(
            pltpu.VMEM((devices, LANES), jnp.int32),
            pltpu.VMEM((samples, LANES), jnp.int32),
        ),
        compiler_params=pltpu.CompilerParams(vmem_limit_bytes=16 * 2**20),
        cost_estimate=pl.CostEstimate(flops=10**10, bytes_accessed=10**8, transcendentals=0),
        name="route",
    )(bag_index, bag_length.T)
    wanted = lax.all_to_all(message, ("rows", "cols"), split_axis=0, concat_axis=0, tiled=True)
    found, select, base, need = pl.pallas_call(
        functools.partial(fetch_kernel, capacity=capacity, small=small, rolled=rolled),
        out_shape=(
            pltpu.VMEM((places, width), jnp.float32),
            pltpu.VMEM((samples * NT, places), jnp.bfloat16),
            pltpu.VMEM((samples, units), jnp.float32),
            pltpu.VMEM((8, LANES), jnp.int32),
        ),
        in_specs=[vmem] * 6,
        out_specs=(vmem,) * 4,
        scratch_shapes=[
            pltpu.SMEM((devices, LANES), jnp.int32),
            pltpu.VMEM((devices * capacity // LANES, 1, LANES), jnp.int32),
            pltpu.VMEM((LANES if rolled else devices * capacity, width), jnp.float32),
            pltpu.SemaphoreType.DMA,
        ],
        compiler_params=pltpu.CompilerParams(vmem_limit_bytes=(40 if rolled else 16) * 2**20),
        name="fetch",
    )(
        wanted,
        place,
        dense_feats,
        w_dense,
        top_bias.reshape(1, units),
        emb_tables.reshape(NT * local_rows, 1, width),
    )
    fetched = lax.all_to_all(
        found.reshape(places, 1, width),
        ("rows", "cols"),
        split_axis=0,
        concat_axis=0,
        tiled=True,
    )
    return pl.pallas_call(
        functools.partial(pool_kernel, small=small),
        out_shape=(
            jax.ShapeDtypeStruct((samples * NT, width), jnp.float32),
            jax.ShapeDtypeStruct((samples, units), jnp.float32),
            jax.ShapeDtypeStruct((1,), jnp.int32),
        ),
        in_specs=[vmem] * 6,
        out_specs=(vmem, vmem, pl.BlockSpec(memory_space=pltpu.SMEM)),
        compiler_params=pltpu.CompilerParams(vmem_limit_bytes=16 * 2**20),
        name="pool",
    )(fetched.reshape(places, width), select, dense_feats, base, w_pair, need)


def shards(*args):
    samples = args[0].shape[0]
    capacity = 2 * samples * NT * L // (lax.axis_size("rows") * lax.axis_size("cols"))
    pooled, hidden, over = exchange(*args, small=SMALL, rolled=False)
    args = lax.optimization_barrier((*args, over))[:-1]
    pooled, hidden = lax.cond(
        over[0] > 0,
        lambda p, h: exchange(*args, small=capacity, rolled=True)[:2],
        lambda p, h: (p, h),
        pooled,
        hidden,
    )
    return pooled.reshape(samples, NT, -1), hidden


def solution(mesh):
    in_specs = (
        P(("rows", "cols"), None),
        P(("rows", "cols"), None),
        P(None, ("rows", "cols"), None),
        P(("rows", "cols"), None),
        P(),
        P(),
        P(),
    )
    out_specs = (P(("rows", "cols"), None, None), P(("rows", "cols"), None))
    return jax.shard_map(shards, mesh=mesh, in_specs=in_specs, out_specs=out_specs, check_vma=False)
```

time: 63 us -> 61.2 us (0.971)
  blocking collectives: 55.4 us -> 51.2 us
  Pallas kernels: 5.91 us -> 8.33 us
  local copies, waits for them, and re-layouts: 0.78 us -> 0.05 us
  between operations: 0.71 us -> 1.42 us
    all_to_all x2, blocking collectives: 55.4 us -> 51.2 us  [the longest x1 30.4 us: exchange(): lax.all_to_all(found.reshape(places, 1, width), ('rows', 'cols'), split_a...]
    pallas_call x3, Pallas kernels: 5.91 us -> 8.33 us  [the longest x1 4.72 us: exchange(): pl.pallas_call(functools.partial(fetch_kernel, capacity=capacity, small=s...]
    unnamed x16 -> x20, local copies, waits for them, and re-layouts: 0.78 us -> 0.05 us
where the time goes in v3:
time: 61.2 us; the launch traced here: 61 us
  blocking collectives  51.2 us (84%)
  Pallas kernels  8.33 us (14%)
  between operations  1.42 us (2%)
    all_to_all x1, blocking collectives, exchange(): lax.all_to_all(found.reshape(places, 1, width), ('rows', 'cols'), split_a...  30.4 us
    all_to_all x1, blocking collectives, exchange(): lax.all_to_all(message, ('rows', 'cols'), split_axis=0, concat_axis=0, ti...  20.8 us
    pallas_call x1, Pallas kernels, exchange(): pl.pallas_call(functools.partial(fetch_kernel, capacity=capacity, small=s...  4.72 us
    pallas_call x1, Pallas kernels, exchange(): pl.pallas_call(functools.partial(route_kernel, local_rows=local_rows, dev...  2.39 us

profile of v3, /device:TPU:1, one launch (start us, length us, event | category | flops | bytes accessed | tf_op | source)
XLA Modules:
  0.0 61.0 jit_solution(1328841506051137426)
XLA Ops:
  0.6 0.0 slice-start
  0.6 0.0 slice-start.1
  0.7 0.0 slice-start.2
  0.7 0.0 slice-start.3
  0.7 0.0 copy-start.1
  0.7 0.0 copy-start.3
  0.7 0.0 copy-start.4
  0.7 2.4 %route.3 = (s32[128,128]{1,0:T(8,128)S(1)}, s32[16,128]{1,0:T(8,128)S(1)}) custom-call(s32[16,128]{1,0:T(8,128)} %idx_ref.1, s32[4,16]{1,0:T(4,128)} %bitcast.39), custom_call_target="tpu_custom_call" | custom-call | flops 10000000000 | bytes 100000000 | tf_op jit(solution)/shard_map/route/pallas_call | solution.py:231
  3.1 20.8 %all_to_all.30 = s32[128,1,128]{2,1,0:T(1,128)S(1)} all-to-all(s32[128,1,128]{2,1,0:T(1,128)S(1)} %bitcast.30), channel_id=1, replica_groups=mesh['rows'=16,'cols'=8] {'rows','cols'}, dimensions={0} | all-to-all | bytes 131072 | tf_op jit(solution)/shard_map/all_to_all | solution.py:243
  23.9 0.0 slice-done
  23.9 0.0 slice-done.1
  23.9 0.0 slice-done.2
  23.9 0.0 slice-done.3
  23.9 0.0 copy-done.1
  23.9 0.0 copy-done.3
  23.9 0.0 copy-done.4
  24.0 4.7 %fetch.3 = (f32[3328,128]{1,0:T(8,128)S(1)}, bf16[64,3328]{1,0:T(8,128)(2,1)S(1)}, f32[16,1024]{1,0:T(8,128)S(1)}, s32[8,128]{1,0:T(8,128)S(1)}) custom-call(s32[128,128]{1,0:T(8,128)S(1)} %bitcast.28, s32[16,128]{1,0:T(8,128)S(1)} %get-tuple-element.59.place_ref, f32[16,128]{1,0:T(8,128)S(1)} %copy-done.3, f32[128,1024]{1,0:T(8,128)S(1)} %copy-done.1, ...), custom_call_target="tpu_custom_call" | custom-call | tf_op jit(solution)/shard_map/fetch/pallas_call | solution.py:244
  28.7 0.0 copy-start.2
  28.7 0.0 copy-start.5
  28.7 0.0 copy-start.6
  28.7 30.4 %all_to_all.31 = f32[3328,1,128]{2,1,0:T(1,128)S(1)} all-to-all(f32[3328,1,128]{2,1,0:T(1,128)S(1)} %bitcast.27), channel_id=1, replica_groups=mesh['rows'=16,'cols'=8] {'rows','cols'}, dimensions={0} | all-to-all | bytes 3407872 | tf_op jit(solution)/shard_map/all_to_all | solution.py:270
  59.1 0.0 copy-done.2
  59.1 1.2 %pool.3 = (f32[64,128]{1,0:T(8,128)}, f32[16,1024]{1,0:T(8,128)}, s32[1]{0:T(128)}) custom-call(f32[3328,128]{1,0:T(8,128)S(1)} %bitcast.25, bf16[64,3328]{1,0:T(8,128)(2,1)S(1)} %get-tuple-element.61.select_ref, f32[16,128]{1,0:T(8,128)S(1)} %copy-done.3, f32[16,1024]{1,0:T(8,128)S(1)} %get-tuple-element.62.base_ref, f32[10,1024]{1,0:T(8,128)S(1)} %copy-done.2, ...), custom_call_target="tpu_custom_call" | custom-call | tf_op jit(solution)/shard_map/pool/pallas_call | solution.py:277
  61.0 0.0 copy-done.5
  61.0 0.0 copy-done.6
  (2 shorter events, 0.0 us)
Async XLA Ops:
  0.6 23.3 %slice-start = ((s8[16777216]{0:T(1024)(128)(4,1)}), s8[4194304]{0:T(1024)(128)(4,1)S(1)}, s32[]{:S(2)}) async-start(s8[16777216]{0:T(1024)(128)(4,1)} %bitcast.32), calls=%async_computation.4 | async-start | bytes 8388608
  0.6 23.3 %slice-start.1 = ((s8[16777216]{0:T(1024)(128)(4,1)}), s8[4194304]{0:T(1024)(128)(4,1)S(1)}, s32[]{:S(2)}) async-start(s8[16777216]{0:T(1024)(128)(4,1)} %bitcast.32), calls=%async_computation.5 | async-start | bytes 8388608
  0.7 23.3 %slice-start.2 = ((s8[16777216]{0:T(1024)(128)(4,1)}), s8[4194304]{0:T(1024)(128)(4,1)S(1)}, s32[]{:S(2)}) async-start(s8[16777216]{0:T(1024)(128)(4,1)} %bitcast.32), calls=%async_computation.6 | async-start | bytes 8388608
  0.7 23.3 %slice-start.3 = ((s8[16777216]{0:T(1024)(128)(4,1)}), s8[4194304]{0:T(1024)(128)(4,1)S(1)}, s32[]{:S(2)}) async-start(s8[16777216]{0:T(1024)(128)(4,1)} %bitcast.32), calls=%async_computation.7 | async-start | bytes 8388608
  0.7 23.3 %copy-start.1 = (f32[128,1024]{1,0:T(8,128)S(1)}, f32[128,1024]{1,0:T(8,128)}, u32[]{:S(2)}) copy-start(f32[128,1024]{1,0:T(8,128)} %wdense_ref.1) | copy-start | bytes 1572868
  0.7 23.3 %copy-start.3 = (f32[16,128]{1,0:T(8,128)S(1)}, f32[16,128]{1,0:T(8,128)}, u32[]{:S(2)}) copy-start(f32[16,128]{1,0:T(8,128)} %dense_ref.3) | copy-start | bytes 24580
  0.7 23.3 %copy-start.4 = (f32[1024]{0:T(1024)S(1)}, f32[1024]{0:T(1024)}, u32[]{:S(2)}) copy-start(f32[1024]{0:T(1024)} %param.15) | copy-start | bytes 12292
  28.7 30.4 %copy-start.2 = (f32[10,1024]{1,0:T(8,128)S(1)}, f32[10,1024]{1,0:T(8,128)}, u32[]{:S(2)}) copy-start(f32[10,1024]{1,0:T(8,128)} %wpair_ref.1) | copy-start | bytes 122884
  28.7 32.3 %copy-start.5 = (s32[16,128]{1,0:T(8,128)S(1)}, s32[16,128]{1,0:T(8,128)}, u32[]{:S(2)}) copy-start(s32[16,128]{1,0:T(8,128)} %idx_ref.1) | copy-start | bytes 24580
  28.7 32.3 %copy-start.6 = (s32[16,4]{0,1:T(4,128)S(1)}, s32[16,4]{0,1:T(4,128)}, u32[]{:S(2)}) copy-start(s32[16,4]{0,1:T(4,128)} %param.10) | copy-start | bytes 772

commit v4 on v3

--- a/solution.py
+++ b/solution.py
@@ -10,7 +10,10 @@
 NT = 4
 L = 32
 LANES = 128
-SMALL = 26
+SMALL = 25
+BLOCK = 8
+CHUNKS = 2
+LAG = 0
 BOTH_LANES = (((1,), (1,)), ((), ()))
 
 
@@ -38,45 +41,39 @@
     high = (code & -256).astype(jnp.float32)
     low = (code & 255).astype(jnp.float32)
 
+    repeat = jnp.zeros((samples, LANES), jnp.int32)
+    for k in range(1, L):
+        same = (pltpu.roll(target, k, axis=1) == target) & (lane % L >= k)
+        repeat = jnp.where(same, 1, repeat)
+    leader = jnp.where(repeat == 0, target, -1)
+
     owner = iota((devices, LANES), 0)
+    row = iota((2 * LANES, LANES), 0)
+    column = iota((2 * LANES, LANES), 1)
+    whole = row >= LANES
+
+    def running(marks, mask):
+        seen = jnp.zeros((devices, LANES), jnp.float32)
+        stack = []
+        for mark in marks:
+            stack.append(jnp.concatenate([mark, seen], axis=1).astype(jnp.bfloat16))
+            seen = seen + mark
+        counter = ones_where(mask | whole).astype(jnp.bfloat16)
+        return jnp.dot(
+            jnp.concatenate(stack, axis=0), counter, preferred_element_type=jnp.float32
+        ), seen
+
     hots = [ones_where(owner == target[i : i + 1, :]) for i in range(samples)]
-    row = iota((LANES, LANES), 0)
-    column = iota((LANES, LANES), 1)
-    ones = jnp.ones((LANES, LANES), jnp.float32)
-    counter = jnp.concatenate(
-        [
-            ones_where(row < column),
-            ones,
-            ones_where((row < column) & (row // L == column // L)),
-        ],
-        axis=1,
-    ).astype(jnp.bfloat16)
-    counts = jnp.dot(
-        jnp.concatenate(hots, axis=0).astype(jnp.bfloat16),
-        counter,
-        preferred_element_type=jnp.float32,
-    )
-    firsts = [
-        jnp.where(counts[i * devices : (i + 1) * devices, 2 * LANES :] == 0.0, hots[i], 0.0)
-        for i in range(samples)
-    ]
-    groups = jnp.dot(
-        jnp.concatenate(firsts, axis=0).astype(jnp.bfloat16),
-        jnp.concatenate([ones_where(row <= column), ones], axis=1).astype(jnp.bfloat16),
-        preferred_element_type=jnp.float32,
-    )
+    firsts = [ones_where(owner == leader[i : i + 1, :]) for i in range(samples)]
+    counts, _ = running(hots, row < column)
+    groups, seen = running(firsts, row <= column)
     slot = iota((capacity, LANES), 0).astype(jnp.float32)
-    before = jnp.zeros((devices, LANES), jnp.float32)
-    groups_before = jnp.zeros((devices, LANES), jnp.float32)
     uppers, lowers = [], []
     for i in range(samples):
         block = counts[i * devices : (i + 1) * devices]
         group = groups[i * devices : (i + 1) * devices]
-        rank = jnp.sum(hots[i] * (block[:, :LANES] + before), axis=0, keepdims=True)
-        which = jnp.sum(hots[i] * (group[:, :LANES] + groups_before), axis=0, keepdims=True)
-        first = jnp.sum(firsts[i], axis=0, keepdims=True)
-        before = before + block[:, LANES : 2 * LANES]
-        groups_before = groups_before + group[:, LANES:]
+        rank = jnp.sum(hots[i] * block, axis=0, keepdims=True)
+        which = jnp.sum(hots[i] * group, axis=0, keepdims=True)
         here = slot == rank
         uppers.append(
             jnp.concatenate(
@@ -85,7 +82,9 @@
         )
         lowers.append(jnp.where(here, low[i : i + 1, :], 0.0).astype(jnp.bfloat16))
         own = target[i : i + 1, :] * small + which.astype(jnp.int32) - 1
-        place_ref[i : i + 1, :] = jnp.where((first > 0.0) & (which <= small), own, -1)
+        place_ref[i : i + 1, :] = jnp.where(
+            (leader[i : i + 1, :] >= 0) & (which <= small), own, -1
+        )
     hot_wide = jnp.concatenate([h.astype(jnp.bfloat16) for h in hots], axis=1)
     slots = samples * LANES
     upper = jnp.concatenate(
@@ -99,7 +98,7 @@
     box = lax.dot_general(
         hot_wide, upper, BOTH_LANES, preferred_element_type=jnp.float32
     ) + lax.dot_general(hot_wide, lower, BOTH_LANES, preferred_element_type=jnp.float32)
-    need = jnp.max(groups_before, axis=0, keepdims=True)
+    need = jnp.max(jnp.sum(seen, axis=1, keepdims=True), axis=0, keepdims=True)
     message_ref[...] = jnp.where(
         iota((devices, LANES), 1) < 2 * capacity, box, need
     ).astype(jnp.int32)
@@ -107,28 +106,41 @@
 
 def fetch_kernel(
     wanted_ref, place_ref, dense_ref, wdense_ref, bias_ref, table_ref,
-    out_ref, select_ref, base_ref, need_ref, ids_ref, key_ref, rows_ref, sem,
+    out_ref, select_ref, base_ref, need_ref, ids_ref, key_ref, rows_ref, sems,
     *, capacity, small, rolled,
 ):
-    copy = pltpu.make_async_copy(wanted_ref, ids_ref, sem)
-    copy.start()
     devices = wanted_ref.shape[0]
+    chunk = devices // CHUNKS
+    copies = [
+        pltpu.make_async_copy(
+            wanted_ref.at[pl.ds(k * chunk, chunk)], ids_ref.at[pl.ds(k * chunk, chunk)], sems.at[k]
+        )
+        for k in range(CHUNKS)
+    ]
+    for copy in copies:
+        copy.start()
     samples = place_ref.shape[0]
-    per_block = LANES // capacity
-    blocks = devices // per_block
-    rows_out = per_block * small
+    wide = BLOCK * capacity
+    blocks = devices // BLOCK
+    rows_out = BLOCK * small
 
     wanted = wanted_ref[...]
     need = jnp.max(
         jnp.where(iota((devices, LANES), 1) < 2 * capacity, 0, wanted), axis=0, keepdims=True
     )
     need_ref[...] = jnp.broadcast_to(need, need_ref.shape)
-    keys = jnp.zeros((blocks, LANES), jnp.int32)
-    for k in range(per_block):
-        which = wanted_ref[pl.ds(k, blocks, stride=per_block), :]
-        which = pltpu.roll(which, (k - 1) * capacity % LANES, axis=1)
-        which = jnp.where((which > 0) & (which <= small), which + (k * small - 1), -1)
-        keys = jnp.where(iota((blocks, LANES), 1) // capacity == k, which, keys)
+    per_row = LANES // capacity
+    halves = []
+    for h in range(BLOCK // per_row):
+        keys = jnp.zeros((blocks, LANES), jnp.int32)
+        for k in range(per_row):
+            src = h * per_row + k
+            which = wanted_ref[pl.ds(src, blocks, stride=BLOCK), :]
+            which = pltpu.roll(which, (k - 1) * capacity % LANES, axis=1)
+            which = jnp.where((which > 0) & (which <= small), which + (src * small - 1), -1)
+            keys = jnp.where(iota((blocks, LANES), 1) // capacity == k, which, keys)
+        halves.append(keys)
+    keys = jnp.concatenate(halves, axis=1)
     for b in range(blocks):
         key_ref[b] = keys[b : b + 1, :]
 
@@ -163,17 +175,18 @@
         )
         + bias_ref[...]
     )
-    copy.wait()
-
-    def one(b, hold):
-        for k in range(per_block):
+
+    def load(b, hold):
+        for k in range(BLOCK):
             for c in range(capacity):
                 at = hold + k * capacity + c
-                rows_ref[at : at + 1, :] = table_ref[ids_ref[b * per_block + k, c]]
-        rows = rows_ref[hold : hold + LANES, :]
+                rows_ref[at : at + 1, :] = table_ref[ids_ref[b * BLOCK + k, c]]
+
+    def reduce(b, hold):
+        rows = rows_ref[hold : hold + wide, :]
         top = rows.astype(jnp.bfloat16)
         rest = (rows - top.astype(jnp.float32)).astype(jnp.bfloat16)
-        gather = ones_where(iota((rows_out, LANES), 0) == key_ref[b]).astype(jnp.bfloat16)
+        gather = ones_where(iota((rows_out, wide), 0) == key_ref[b]).astype(jnp.bfloat16)
         sums = jnp.dot(
             gather, jnp.concatenate([top, rest], axis=1), preferred_element_type=jnp.float32
         )
@@ -181,10 +194,18 @@
         out_ref[pl.ds(start, rows_out), :] = sums[:, :LANES] + sums[:, LANES:]
 
     if rolled:
-        lax.fori_loop(0, blocks, lambda b, carry: (one(b, 0), carry)[1], 0)
+        for copy in copies:
+            copy.wait()
+        lax.fori_loop(0, blocks, lambda b, carry: (load(b, 0), reduce(b, 0), carry)[2], 0)
     else:
         for b in range(blocks):
-            one(b, b * LANES)
+            if b * BLOCK % chunk == 0:
+                copies[b * BLOCK // chunk].wait()
+            load(b, b * wide)
+            if b >= LAG:
+                reduce(b - LAG, (b - LAG) * wide)
+        for b in range(blocks - LAG, blocks):
+            reduce(b, b * wide)
 
 
 def pool_kernel(
@@ -253,9 +274,9 @@
         out_specs=(vmem,) * 4,
         scratch_shapes=[
             pltpu.SMEM((devices, LANES), jnp.int32),
-            pltpu.VMEM((devices * capacity // LANES, 1, LANES), jnp.int32),
-            pltpu.VMEM((LANES if rolled else devices * capacity, width), jnp.float32),
-            pltpu.SemaphoreType.DMA,
+            pltpu.VMEM((devices // BLOCK, 1, BLOCK * capacity), jnp.int32),
+            pltpu.VMEM(((BLOCK if rolled else devices) * capacity, width), jnp.float32),
+            pltpu.SemaphoreType.DMA((CHUNKS,)),
         ],
         compiler_params=pltpu.CompilerParams(vmem_limit_bytes=(40 if rolled else 16) * 2**20),
         name="fetch",
@@ -279,7 +300,7 @@
         out_shape=(
             jax.ShapeDtypeStruct((samples * NT, width), jnp.float32),
             jax.ShapeDtypeStruct((samples, units), jnp.float32),
-            jax.ShapeDtypeStruct((1,), jnp.int32),
+            pltpu.SMEM((1,), jnp.int32),
         ),
         in_specs=[vmem] * 6,
         out_specs=(vmem, vmem, pl.BlockSpec(memory_space=pltpu.SMEM)),
@@ -293,10 +314,9 @@
     capacity = 2 * samples * NT * L // (lax.axis_size("rows") * lax.axis_size("cols"))
     pooled, hidden, over = exchange(*args, small=SMALL, rolled=False)
     args = lax.optimization_barrier((*args, over))[:-1]
-    pooled, hidden = lax.cond(
-        over[0] > 0,
-        lambda p, h: exchange(*args, small=capacity, rolled=True)[:2],
-        lambda p, h: (p, h),
+    pooled, hidden = lax.switch(
+        over[0],
+        (lambda p, h: (p, h), lambda p, h: exchange(*args, small=capacity, rolled=True)[:2]),
         pooled,
         hidden,
     )

time: 61.2 us -> 59.7 us (0.975)
  between operations: 1.42 us -> 0.77 us
    all_to_all x1, blocking collectives: 30.4 us -> 29.7 us  [exchange(): lax.all_to_all(found.reshape(places, 1, width), ('rows', 'cols'), split_a...]
where the time goes in v4:
time: 59.7 us; the launch traced here: 59.5 us
  blocking collectives  50.6 us (85%)
  Pallas kernels  8.14 us (14%)
  between operations  0.77 us (1%)
    all_to_all x1, blocking collectives, exchange(): lax.all_to_all(found.reshape(places, 1, width), ('rows', 'cols'), split_a...  29.7 us
    all_to_all x1, blocking collectives, exchange(): lax.all_to_all(message, ('rows', 'cols'), split_axis=0, concat_axis=0, ti...  20.8 us
    pallas_call x1, Pallas kernels, exchange(): pl.pallas_call(functools.partial(fetch_kernel, capacity=capacity, small=s...  4.58 us
    pallas_call x1, Pallas kernels, exchange(): pl.pallas_call(functools.partial(route_kernel, local_rows=local_rows, dev...  2.37 us

profile of v4, /device:TPU:1, one launch (start us, length us, event | category | flops | bytes accessed | tf_op | source)
XLA Modules:
  0.0 59.5 jit_solution(3955472500906676558)
XLA Ops:
  0.6 0.0 slice-start
  0.6 0.0 slice-start.1
  0.7 0.0 slice-start.2
  0.7 0.0 slice-start.3
  0.7 0.0 copy-start.1
  0.7 0.0 copy-start.3
  0.7 0.0 copy-start.4
  0.7 2.4 %route.3 = (s32[128,128]{1,0:T(8,128)S(1)}, s32[16,128]{1,0:T(8,128)S(1)}) custom-call(s32[16,128]{1,0:T(8,128)} %idx_ref.1, s32[4,16]{1,0:T(4,128)} %bitcast.39), custom_call_target="tpu_custom_call" | custom-call | flops 10000000000 | bytes 100000000 | tf_op jit(solution)/shard_map/route/pallas_call | solution.py:252
  3.1 20.8 %all_to_all.30 = s32[128,1,128]{2,1,0:T(1,128)S(1)} all-to-all(s32[128,1,128]{2,1,0:T(1,128)S(1)} %bitcast.30), channel_id=1, replica_groups=mesh['rows'=16,'cols'=8] {'rows','cols'}, dimensions={0} | all-to-all | bytes 131072 | tf_op jit(solution)/shard_map/all_to_all | solution.py:264
  23.9 0.0 slice-done
  23.9 0.0 slice-done.1
  23.9 0.0 slice-done.2
  23.9 0.0 slice-done.3
  23.9 0.0 copy-done.1
  23.9 0.0 copy-done.3
  23.9 0.0 copy-done.4
  24.0 4.6 %fetch.3 = (f32[3200,128]{1,0:T(8,128)S(1)}, bf16[64,3200]{1,0:T(8,128)(2,1)S(1)}, f32[16,1024]{1,0:T(8,128)S(1)}, s32[8,128]{1,0:T(8,128)S(1)}) custom-call(s32[128,128]{1,0:T(8,128)S(1)} %bitcast.28, s32[16,128]{1,0:T(8,128)S(1)} %get-tuple-element.59.place_ref, f32[16,128]{1,0:T(8,128)S(1)} %copy-done.3, f32[128,1024]{1,0:T(8,128)S(1)} %copy-done.1, ...), custom_call_target="tpu_custom_call" | custom-call | tf_op jit(solution)/shard_map/fetch/pallas_call | solution.py:265
  28.5 0.0 copy-start.2
  28.6 0.0 copy-start.5
  28.6 0.0 copy-start.6
  28.6 29.7 %all_to_all.31 = f32[3200,1,128]{2,1,0:T(1,128)S(1)} all-to-all(f32[3200,1,128]{2,1,0:T(1,128)S(1)} %bitcast.27), channel_id=1, replica_groups=mesh['rows'=16,'cols'=8] {'rows','cols'}, dimensions={0} | all-to-all | bytes 3276800 | tf_op jit(solution)/shard_map/all_to_all | solution.py:291
  58.3 0.0 copy-done.2
  58.3 1.2 %pool.3 = (f32[64,128]{1,0:T(8,128)}, f32[16,1024]{1,0:T(8,128)}, s32[1]{0:T(128)S(4)}) custom-call(f32[3200,128]{1,0:T(8,128)S(1)} %bitcast.25, bf16[64,3200]{1,0:T(8,128)(2,1)S(1)} %get-tuple-element.61.select_ref, f32[16,128]{1,0:T(8,128)S(1)} %copy-done.3, f32[16,1024]{1,0:T(8,128)S(1)} %get-tuple-element.62.base_ref, f32[10,1024]{1,0:T(8,128)S(1)} %copy-done.2, ...), custom_call_target="tpu_custom_call" | custom-call | tf_op jit(solution)/shard_map/pool/pallas_call | solution.py:298
  59.5 0.0 copy-done.5
  59.5 0.0 copy-done.6
  (2 shorter events, 0.0 us)
Async XLA Ops:
  0.6 23.3 %slice-start = ((s8[16777216]{0:T(1024)(128)(4,1)}), s8[4194304]{0:T(1024)(128)(4,1)S(1)}, s32[]{:S(2)}) async-start(s8[16777216]{0:T(1024)(128)(4,1)} %bitcast.32), calls=%async_computation.4 | async-start | bytes 8388608
  0.6 23.3 %slice-start.1 = ((s8[16777216]{0:T(1024)(128)(4,1)}), s8[4194304]{0:T(1024)(128)(4,1)S(1)}, s32[]{:S(2)}) async-start(s8[16777216]{0:T(1024)(128)(4,1)} %bitcast.32), calls=%async_computation.5 | async-start | bytes 8388608
  0.7 23.3 %slice-start.2 = ((s8[16777216]{0:T(1024)(128)(4,1)}), s8[4194304]{0:T(1024)(128)(4,1)S(1)}, s32[]{:S(2)}) async-start(s8[16777216]{0:T(1024)(128)(4,1)} %bitcast.32), calls=%async_computation.6 | async-start | bytes 8388608
  0.7 23.2 %slice-start.3 = ((s8[16777216]{0:T(1024)(128)(4,1)}), s8[4194304]{0:T(1024)(128)(4,1)S(1)}, s32[]{:S(2)}) async-start(s8[16777216]{0:T(1024)(128)(4,1)} %bitcast.32), calls=%async_computation.7 | async-start | bytes 8388608
  0.7 23.2 %copy-start.1 = (f32[128,1024]{1,0:T(8,128)S(1)}, f32[128,1024]{1,0:T(8,128)}, u32[]{:S(2)}) copy-start(f32[128,1024]{1,0:T(8,128)} %wdense_ref.1) | copy-start | bytes 1572868
  0.7 23.2 %copy-start.3 = (f32[16,128]{1,0:T(8,128)S(1)}, f32[16,128]{1,0:T(8,128)}, u32[]{:S(2)}) copy-start(f32[16,128]{1,0:T(8,128)} %dense_ref.3) | copy-start | bytes 24580
  0.7 23.2 %copy-start.4 = (f32[1024]{0:T(1024)S(1)}, f32[1024]{0:T(1024)}, u32[]{:S(2)}) copy-start(f32[1024]{0:T(1024)} %param.15) | copy-start | bytes 12292
  28.5 29.8 %copy-start.2 = (f32[10,1024]{1,0:T(8,128)S(1)}, f32[10,1024]{1,0:T(8,128)}, u32[]{:S(2)}) copy-start(f32[10,1024]{1,0:T(8,128)} %wpair_ref.1) | copy-start | bytes 122884
  28.6 31.0 %copy-start.5 = (s32[16,128]{1,0:T(8,128)S(1)}, s32[16,128]{1,0:T(8,128)}, u32[]{:S(2)}) copy-start(s32[16,128]{1,0:T(8,128)} %idx_ref.1) | copy-start | bytes 24580
  28.6 30.9 %copy-start.6 = (s32[16,4]{0,1:T(4,128)S(1)}, s32[16,4]{0,1:T(4,128)}, u32[]{:S(2)}) copy-start(s32[16,4]{0,1:T(4,128)} %param.10) | copy-start | bytes 772

commit v5 on v4

--- a/solution.py
+++ b/solution.py
@@ -41,66 +41,73 @@
     high = (code & -256).astype(jnp.float32)
     low = (code & 255).astype(jnp.float32)
 
+    ahead = [
+        (pltpu.roll(target, k, axis=1) == target) & (lane % L >= k) for k in range(1, L)
+    ]
     repeat = jnp.zeros((samples, LANES), jnp.int32)
-    for k in range(1, L):
-        same = (pltpu.roll(target, k, axis=1) == target) & (lane % L >= k)
+    for same in ahead:
         repeat = jnp.where(same, 1, repeat)
     leader = jnp.where(repeat == 0, target, -1)
 
     owner = iota((devices, LANES), 0)
-    row = iota((2 * LANES, LANES), 0)
-    column = iota((2 * LANES, LANES), 1)
-    whole = row >= LANES
-
-    def running(marks, mask):
-        seen = jnp.zeros((devices, LANES), jnp.float32)
-        stack = []
+    row = iota((LANES, LANES), 0)
+    column = iota((LANES, LANES), 1)
+    earlier = ones_where(row < column).astype(jnp.bfloat16)
+
+    def numbers(targets):
+        marks = [ones_where(owner == targets[i : i + 1, :]) for i in range(samples)]
+        seen = marks[0]
+        for mark in marks[1:]:
+            seen = seen + mark
+        running = jnp.dot(
+            seen.astype(jnp.bfloat16), earlier, preferred_element_type=jnp.float32
+        )
+        found = []
         for mark in marks:
-            stack.append(jnp.concatenate([mark, seen], axis=1).astype(jnp.bfloat16))
-            seen = seen + mark
-        counter = ones_where(mask | whole).astype(jnp.bfloat16)
-        return jnp.dot(
-            jnp.concatenate(stack, axis=0), counter, preferred_element_type=jnp.float32
-        ), seen
-
-    hots = [ones_where(owner == target[i : i + 1, :]) for i in range(samples)]
-    firsts = [ones_where(owner == leader[i : i + 1, :]) for i in range(samples)]
-    counts, _ = running(hots, row < column)
-    groups, seen = running(firsts, row <= column)
+            found.append(jnp.sum(mark * running, axis=0, keepdims=True))
+            running = running + mark
+        return marks, found, seen
+
+    hots, ranks, _ = numbers(target)
+    _, orders, seen = numbers(leader)
+    order = jnp.concatenate(orders, axis=0)
+    which = order
+    for k, same in enumerate(ahead, 1):
+        lead = pltpu.roll(leader, k, axis=1) >= 0
+        which = jnp.where(same & lead, pltpu.roll(order, k, axis=1), which)
+    which = which + 1.0
     slot = iota((capacity, LANES), 0).astype(jnp.float32)
-    uppers, lowers = [], []
+    pieces = []
     for i in range(samples):
-        block = counts[i * devices : (i + 1) * devices]
-        group = groups[i * devices : (i + 1) * devices]
-        rank = jnp.sum(hots[i] * block, axis=0, keepdims=True)
-        which = jnp.sum(hots[i] * group, axis=0, keepdims=True)
-        here = slot == rank
-        uppers.append(
+        here = slot == ranks[i]
+        pieces.append(
             jnp.concatenate(
-                [jnp.where(here, high[i : i + 1, :], 0.0), jnp.where(here, which, 0.0)], axis=0
+                [
+                    jnp.where(here, value[i : i + 1, :], 0.0)
+                    for value in (high, which, low)
+                ]
+                + [jnp.zeros((LANES - 3 * capacity, LANES), jnp.float32)],
+                axis=0,
             ).astype(jnp.bfloat16)
         )
-        lowers.append(jnp.where(here, low[i : i + 1, :], 0.0).astype(jnp.bfloat16))
-        own = target[i : i + 1, :] * small + which.astype(jnp.int32) - 1
-        place_ref[i : i + 1, :] = jnp.where(
-            (leader[i : i + 1, :] >= 0) & (which <= small), own, -1
-        )
+    number = which.astype(jnp.int32)
+    place_ref[...] = jnp.where(
+        (leader >= 0) & (number <= small), target * small + number - 1, -1
+    )
     hot_wide = jnp.concatenate([h.astype(jnp.bfloat16) for h in hots], axis=1)
-    slots = samples * LANES
-    upper = jnp.concatenate(
-        [jnp.concatenate(uppers, axis=1), jnp.zeros((LANES - 2 * capacity, slots), jnp.bfloat16)],
-        axis=0,
-    )
-    lower = jnp.concatenate(
-        [jnp.concatenate(lowers, axis=1), jnp.zeros((LANES - capacity, slots), jnp.bfloat16)],
-        axis=0,
-    )
     box = lax.dot_general(
-        hot_wide, upper, BOTH_LANES, preferred_element_type=jnp.float32
-    ) + lax.dot_general(hot_wide, lower, BOTH_LANES, preferred_element_type=jnp.float32)
+        hot_wide,
+        jnp.concatenate(pieces, axis=1),
+        BOTH_LANES,
+        preferred_element_type=jnp.float32,
+    )
+    side = iota((devices, LANES), 1)
+    box = box + jnp.where(
+        side < capacity, pltpu.roll(box, LANES - 2 * capacity, axis=1), 0.0
+    )
     need = jnp.max(jnp.sum(seen, axis=1, keepdims=True), axis=0, keepdims=True)
     message_ref[...] = jnp.where(
-        iota((devices, LANES), 1) < 2 * capacity, box, need
+        side < 2 * capacity, box, need
     ).astype(jnp.int32)
 
 

time: 59.7 us -> 59.4 us (level)
  no operation moved by 1% of the time
where the time goes in v5:
time: 59.4 us; the launch traced here: 59.3 us
  blocking collectives  50.5 us (85%)
  Pallas kernels  7.94 us (13%)
  between operations  0.77 us (1%)
    all_to_all x1, blocking collectives, exchange(): lax.all_to_all(found.reshape(places, 1, width), ('rows', 'cols'), split_a...  29.7 us
    all_to_all x1, blocking collectives, exchange(): lax.all_to_all(message, ('rows', 'cols'), split_axis=0, concat_axis=0, ti...  20.8 us
    pallas_call x1, Pallas kernels, exchange(): pl.pallas_call(functools.partial(fetch_kernel, capacity=capacity, small=s...  4.61 us
    pallas_call x1, Pallas kernels, exchange(): pl.pallas_call(functools.partial(route_kernel, local_rows=local_rows, dev...  2.14 us

profile of v5, /device:TPU:1, one launch (start us, length us, event | category | flops | bytes accessed | tf_op | source)
XLA Modules:
  0.0 59.3 jit_solution(1679267417107655036)
XLA Ops:
  0.6 0.0 slice-start
  0.6 0.0 slice-start.1
  0.7 0.0 slice-start.2
  0.7 0.0 slice-start.3
  0.7 0.0 copy-start.1
  0.7 0.0 copy-start.3
  0.7 0.0 copy-start.4
  0.7 2.1 %route.3 = (s32[128,128]{1,0:T(8,128)S(1)}, s32[16,128]{1,0:T(8,128)S(1)}) custom-call(s32[16,128]{1,0:T(8,128)} %idx_ref.1, s32[4,16]{1,0:T(4,128)} %bitcast.39), custom_call_target="tpu_custom_call" | custom-call | flops 10000000000 | bytes 100000000 | tf_op jit(solution)/shard_map/route/pallas_call | solution.py:259
  2.9 20.8 %all_to_all.30 = s32[128,1,128]{2,1,0:T(1,128)S(1)} all-to-all(s32[128,1,128]{2,1,0:T(1,128)S(1)} %bitcast.30), channel_id=1, replica_groups=mesh['rows'=16,'cols'=8] {'rows','cols'}, dimensions={0} | all-to-all | bytes 131072 | tf_op jit(solution)/shard_map/all_to_all | solution.py:271
  23.7 0.0 slice-done
  23.7 0.0 slice-done.1
  23.7 0.0 slice-done.2
  23.7 0.0 slice-done.3
  23.7 0.0 copy-done.1
  23.7 0.0 copy-done.3
  23.7 0.0 copy-done.4
  23.7 4.6 %fetch.3 = (f32[3200,128]{1,0:T(8,128)S(1)}, bf16[64,3200]{1,0:T(8,128)(2,1)S(1)}, f32[16,1024]{1,0:T(8,128)S(1)}, s32[8,128]{1,0:T(8,128)S(1)}) custom-call(s32[128,128]{1,0:T(8,128)S(1)} %bitcast.28, s32[16,128]{1,0:T(8,128)S(1)} %get-tuple-element.59.place_ref, f32[16,128]{1,0:T(8,128)S(1)} %copy-done.3, f32[128,1024]{1,0:T(8,128)S(1)} %copy-done.1, ...), custom_call_target="tpu_custom_call" | custom-call | tf_op jit(solution)/shard_map/fetch/pallas_call | solution.py:272
  28.3 0.0 copy-start.2
  28.4 0.0 copy-start.5
  28.4 0.0 copy-start.6
  28.4 29.7 %all_to_all.31 = f32[3200,1,128]{2,1,0:T(1,128)S(1)} all-to-all(f32[3200,1,128]{2,1,0:T(1,128)S(1)} %bitcast.27), channel_id=1, replica_groups=mesh['rows'=16,'cols'=8] {'rows','cols'}, dimensions={0} | all-to-all | bytes 3276800 | tf_op jit(solution)/shard_map/all_to_all | solution.py:298
  58.1 0.0 copy-done.2
  58.1 1.2 %pool.3 = (f32[64,128]{1,0:T(8,128)}, f32[16,1024]{1,0:T(8,128)}, s32[1]{0:T(128)S(4)}) custom-call(f32[3200,128]{1,0:T(8,128)S(1)} %bitcast.25, bf16[64,3200]{1,0:T(8,128)(2,1)S(1)} %get-tuple-element.61.select_ref, f32[16,128]{1,0:T(8,128)S(1)} %copy-done.3, f32[16,1024]{1,0:T(8,128)S(1)} %get-tuple-element.62.base_ref, f32[10,1024]{1,0:T(8,128)S(1)} %copy-done.2, ...), custom_call_target="tpu_custom_call" | custom-call | tf_op jit(solution)/shard_map/pool/pallas_call | solution.py:305
  59.3 0.0 copy-done.5
  59.3 0.0 copy-done.6
  (2 shorter events, 0.0 us)
Async XLA Ops:
  0.6 23.0 %slice-start = ((s8[16777216]{0:T(1024)(128)(4,1)}), s8[4194304]{0:T(1024)(128)(4,1)S(1)}, s32[]{:S(2)}) async-start(s8[16777216]{0:T(1024)(128)(4,1)} %bitcast.32), calls=%async_computation.4 | async-start | bytes 8388608
  0.6 23.0 %slice-start.1 = ((s8[16777216]{0:T(1024)(128)(4,1)}), s8[4194304]{0:T(1024)(128)(4,1)S(1)}, s32[]{:S(2)}) async-start(s8[16777216]{0:T(1024)(128)(4,1)} %bitcast.32), calls=%async_computation.5 | async-start | bytes 8388608
  0.7 23.0 %slice-start.2 = ((s8[16777216]{0:T(1024)(128)(4,1)}), s8[4194304]{0:T(1024)(128)(4,1)S(1)}, s32[]{:S(2)}) async-start(s8[16777216]{0:T(1024)(128)(4,1)} %bitcast.32), calls=%async_computation.6 | async-start | bytes 8388608
  0.7 23.0 %slice-start.3 = ((s8[16777216]{0:T(1024)(128)(4,1)}), s8[4194304]{0:T(1024)(128)(4,1)S(1)}, s32[]{:S(2)}) async-start(s8[16777216]{0:T(1024)(128)(4,1)} %bitcast.32), calls=%async_computation.7 | async-start | bytes 8388608
  0.7 23.0 %copy-start.1 = (f32[128,1024]{1,0:T(8,128)S(1)}, f32[128,1024]{1,0:T(8,128)}, u32[]{:S(2)}) copy-start(f32[128,1024]{1,0:T(8,128)} %wdense_ref.1) | copy-start | bytes 1572868
  0.7 23.0 %copy-start.3 = (f32[16,128]{1,0:T(8,128)S(1)}, f32[16,128]{1,0:T(8,128)}, u32[]{:S(2)}) copy-start(f32[16,128]{1,0:T(8,128)} %dense_ref.3) | copy-start | bytes 24580
  0.7 23.0 %copy-start.4 = (f32[1024]{0:T(1024)S(1)}, f32[1024]{0:T(1024)}, u32[]{:S(2)}) copy-start(f32[1024]{0:T(1024)} %param.15) | copy-start | bytes 12292
  28.3 29.8 %copy-start.2 = (f32[10,1024]{1,0:T(8,128)S(1)}, f32[10,1024]{1,0:T(8,128)}, u32[]{:S(2)}) copy-start(f32[10,1024]{1,0:T(8,128)} %wpair_ref.1) | copy-start | bytes 122884
  28.4 30.9 %copy-start.5 = (s32[16,128]{1,0:T(8,128)S(1)}, s32[16,128]{1,0:T(8,128)}, u32[]{:S(2)}) copy-start(s32[16,128]{1,0:T(8,128)} %idx_ref.1) | copy-start | bytes 24580
  28.4 30.9 %copy-start.6 = (s32[16,4]{0,1:T(4,128)S(1)}, s32[16,4]{0,1:T(4,128)}, u32[]{:S(2)}) copy-start(s32[16,4]{0,1:T(4,128)} %param.10) | copy-start | bytes 772

commit v6 on v5

--- a/solution.py
+++ b/solution.py
@@ -12,7 +12,7 @@
 LANES = 128
 SMALL = 25
 BLOCK = 8
-CHUNKS = 2
+CHUNKS = 3
 LAG = 0
 BOTH_LANES = (((1,), (1,)), ((), ()))
 
@@ -117,12 +117,12 @@
     *, capacity, small, rolled,
 ):
     devices = wanted_ref.shape[0]
-    chunk = devices // CHUNKS
+    starts = (0, 2 * BLOCK, devices // 2, devices)
     copies = [
         pltpu.make_async_copy(
-            wanted_ref.at[pl.ds(k * chunk, chunk)], ids_ref.at[pl.ds(k * chunk, chunk)], sems.at[k]
-        )
-        for k in range(CHUNKS)
+            wanted_ref.at[pl.ds(start, end - start)], ids_ref.at[pl.ds(start, end - start)], sems.at[k]
+        )
+        for k, (start, end) in enumerate(zip(starts, starts[1:]))
     ]
     for copy in copies:
         copy.start()
@@ -206,8 +206,8 @@
         lax.fori_loop(0, blocks, lambda b, carry: (load(b, 0), reduce(b, 0), carry)[2], 0)
     else:
         for b in range(blocks):
-            if b * BLOCK % chunk == 0:
-                copies[b * BLOCK // chunk].wait()
+            if b * BLOCK in starts:
+                copies[starts.index(b * BLOCK)].wait()
             load(b, b * wide)
             if b >= LAG:
                 reduce(b - LAG, (b - LAG) * wide)

time: 59.4 us -> 59.3 us (level)
  no operation moved by 1% of the time
where the time goes in v6:
time: 59.3 us; the launch traced here: 59.2 us
  blocking collectives  50.5 us (85%)
  Pallas kernels  7.82 us (13%)
  between operations  0.77 us (1%)
    all_to_all x1, blocking collectives, exchange(): lax.all_to_all(found.reshape(places, 1, width), ('rows', 'cols'), split_a...  29.7 us
    all_to_all x1, blocking collectives, exchange(): lax.all_to_all(message, ('rows', 'cols'), split_axis=0, concat_axis=0, ti...  20.8 us
    pallas_call x1, Pallas kernels, exchange(): pl.pallas_call(functools.partial(fetch_kernel, capacity=capacity, small=s...  4.49 us
    pallas_call x1, Pallas kernels, exchange(): pl.pallas_call(functools.partial(route_kernel, local_rows=local_rows, dev...  2.14 us
    pallas_call x1, Pallas kernels, exchange(): pl.pallas_call(functools.partial(pool_kernel, small=small), out_shape=(ja...  1.19 us

profile of v6, /device:TPU:1, one launch (start us, length us, event | category | flops | bytes accessed | tf_op | source)
XLA Modules:
  0.0 59.2 jit_solution(13013818001583793774)
XLA Ops:
  0.6 0.0 slice-start
  0.6 0.0 slice-start.1
  0.7 0.0 slice-start.2
  0.7 0.0 slice-start.3
  0.7 0.0 copy-start.1
  0.7 0.0 copy-start.3
  0.7 0.0 copy-start.4
  0.7 2.1 %route.3 = (s32[128,128]{1,0:T(8,128)S(1)}, s32[16,128]{1,0:T(8,128)S(1)}) custom-call(s32[16,128]{1,0:T(8,128)} %idx_ref.1, s32[4,16]{1,0:T(4,128)} %bitcast.39), custom_call_target="tpu_custom_call" | custom-call | flops 10000000000 | bytes 100000000 | tf_op jit(solution)/shard_map/route/pallas_call | solution.py:259
  2.9 20.8 %all_to_all.30 = s32[128,1,128]{2,1,0:T(1,128)S(1)} all-to-all(s32[128,1,128]{2,1,0:T(1,128)S(1)} %bitcast.30), channel_id=1, replica_groups=mesh['rows'=16,'cols'=8] {'rows','cols'}, dimensions={0} | all-to-all | bytes 131072 | tf_op jit(solution)/shard_map/all_to_all | solution.py:271
  23.7 0.0 slice-done
  23.7 0.0 slice-done.1
  23.7 0.0 slice-done.2
  23.7 0.0 slice-done.3
  23.7 0.0 copy-done.1
  23.7 0.0 copy-done.3
  23.7 0.0 copy-done.4
  23.7 4.5 %fetch.3 = (f32[3200,128]{1,0:T(8,128)S(1)}, bf16[64,3200]{1,0:T(8,128)(2,1)S(1)}, f32[16,1024]{1,0:T(8,128)S(1)}, s32[8,128]{1,0:T(8,128)S(1)}) custom-call(s32[128,128]{1,0:T(8,128)S(1)} %bitcast.28, s32[16,128]{1,0:T(8,128)S(1)} %get-tuple-element.59.place_ref, f32[16,128]{1,0:T(8,128)S(1)} %copy-done.3, f32[128,1024]{1,0:T(8,128)S(1)} %copy-done.1, ...), custom_call_target="tpu_custom_call" | custom-call | tf_op jit(solution)/shard_map/fetch/pallas_call | solution.py:272
  28.2 0.0 copy-start.2
  28.2 0.0 copy-start.5
  28.2 0.0 copy-start.6
  28.3 29.7 %all_to_all.31 = f32[3200,1,128]{2,1,0:T(1,128)S(1)} all-to-all(f32[3200,1,128]{2,1,0:T(1,128)S(1)} %bitcast.27), channel_id=1, replica_groups=mesh['rows'=16,'cols'=8] {'rows','cols'}, dimensions={0} | all-to-all | bytes 3276800 | tf_op jit(solution)/shard_map/all_to_all | solution.py:298
  58.0 0.0 copy-done.2
  58.0 1.2 %pool.3 = (f32[64,128]{1,0:T(8,128)}, f32[16,1024]{1,0:T(8,128)}, s32[1]{0:T(128)S(4)}) custom-call(f32[3200,128]{1,0:T(8,128)S(1)} %bitcast.25, bf16[64,3200]{1,0:T(8,128)(2,1)S(1)} %get-tuple-element.61.select_ref, f32[16,128]{1,0:T(8,128)S(1)} %copy-done.3, f32[16,1024]{1,0:T(8,128)S(1)} %get-tuple-element.62.base_ref, f32[10,1024]{1,0:T(8,128)S(1)} %copy-done.2, ...), custom_call_target="tpu_custom_call" | custom-call | tf_op jit(solution)/shard_map/pool/pallas_call | solution.py:305
  59.2 0.0 copy-done.5
  59.2 0.0 copy-done.6
  (2 shorter events, 0.0 us)
Async XLA Ops:
  0.6 23.0 %slice-start = ((s8[16777216]{0:T(1024)(128)(4,1)}), s8[4194304]{0:T(1024)(128)(4,1)S(1)}, s32[]{:S(2)}) async-start(s8[16777216]{0:T(1024)(128)(4,1)} %bitcast.32), calls=%async_computation.4 | async-start | bytes 8388608
  0.6 23.0 %slice-start.1 = ((s8[16777216]{0:T(1024)(128)(4,1)}), s8[4194304]{0:T(1024)(128)(4,1)S(1)}, s32[]{:S(2)}) async-start(s8[16777216]{0:T(1024)(128)(4,1)} %bitcast.32), calls=%async_computation.5 | async-start | bytes 8388608
  0.7 23.0 %slice-start.2 = ((s8[16777216]{0:T(1024)(128)(4,1)}), s8[4194304]{0:T(1024)(128)(4,1)S(1)}, s32[]{:S(2)}) async-start(s8[16777216]{0:T(1024)(128)(4,1)} %bitcast.32), calls=%async_computation.6 | async-start | bytes 8388608
  0.7 23.0 %slice-start.3 = ((s8[16777216]{0:T(1024)(128)(4,1)}), s8[4194304]{0:T(1024)(128)(4,1)S(1)}, s32[]{:S(2)}) async-start(s8[16777216]{0:T(1024)(128)(4,1)} %bitcast.32), calls=%async_computation.7 | async-start | bytes 8388608
  0.7 23.0 %copy-start.1 = (f32[128,1024]{1,0:T(8,128)S(1)}, f32[128,1024]{1,0:T(8,128)}, u32[]{:S(2)}) copy-start(f32[128,1024]{1,0:T(8,128)} %wdense_ref.1) | copy-start | bytes 1572868
  0.7 23.0 %copy-start.3 = (f32[16,128]{1,0:T(8,128)S(1)}, f32[16,128]{1,0:T(8,128)}, u32[]{:S(2)}) copy-start(f32[16,128]{1,0:T(8,128)} %dense_ref.3) | copy-start | bytes 24580
  0.7 23.0 %copy-start.4 = (f32[1024]{0:T(1024)S(1)}, f32[1024]{0:T(1024)}, u32[]{:S(2)}) copy-start(f32[1024]{0:T(1024)} %param.15) | copy-start | bytes 12292
  28.2 29.7 %copy-start.2 = (f32[10,1024]{1,0:T(8,128)S(1)}, f32[10,1024]{1,0:T(8,128)}, u32[]{:S(2)}) copy-start(f32[10,1024]{1,0:T(8,128)} %wpair_ref.1) | copy-start | bytes 122884
  28.2 30.9 %copy-start.5 = (s32[16,128]{1,0:T(8,128)S(1)}, s32[16,128]{1,0:T(8,128)}, u32[]{:S(2)}) copy-start(s32[16,128]{1,0:T(8,128)} %idx_ref.1) | copy-start | bytes 24580
  28.2 30.9 %copy-start.6 = (s32[16,4]{0,1:T(4,128)S(1)}, s32[16,4]{0,1:T(4,128)}, u32[]{:S(2)}) copy-start(s32[16,4]{0,1:T(4,128)} %param.10) | copy-start | bytes 772
